TPU v7x, 8 devices: a whole 2x2x1 slice. The times are simulated.
8 devices in a mesh: inst: 1 (over z), qy: 2 (over y), qx: 4 (over x, core).
Axes of the slice: x: 2, y: 2, z: 1, core: 2. Of those that a mesh axis runs over, the one named last changes fastest.
Arguments:
- cost_diag: float32 [2097152], P(('inst', 'qx', 'qy'))
- gammas: float32 [8], replicated
- betas: float32 [8], replicated
Outputs:
- output 1: float32 [1], P('inst')
- output 2: float32 [2097152], P(('inst', 'qx', 'qy'))
- output 3: float32 [2097152], P(('inst', 'qx', 'qy'))
All inputs are finite; a program needn't handle non-finite values.
Results may differ from a plain program's by a relative error of at most 0.001.
Values sent between devices are 32-bit elements.
A program may use at most 1 GiB of HBM per device.

v0:
```python
import math
import jax
import jax.numpy as jnp
from jax import lax
from jax.sharding import PartitionSpec as P

LANES = 128


def quarter_turn(state_pair):
    sign_pair = jnp.array([1.0, -1.0], jnp.float32).reshape(2, 1, 1)
    return jnp.flip(state_pair, axis=0) * sign_pair


def flip_bit(state_pair, qubit_id):
    if qubit_id < 7:
        axis_id = 2
        bit_step = 1 << qubit_id
    else:
        axis_id = 1
        bit_step = 1 << (qubit_id - 7)
    extent = state_pair.shape[axis_id]
    iota_shape = [1, 1, 1]
    iota_shape[axis_id] = extent
    position = lax.broadcasted_iota(jnp.int32, tuple(iota_shape), axis_id)
    bit_set = (position & bit_step) != 0
    return jnp.where(bit_set, jnp.roll(state_pair, bit_step, axis=axis_id),
                     jnp.roll(state_pair, -bit_step, axis=axis_id))


def local_mixer(state_pair, cos_half, sin_half, qubit_ids):
    for qubit_id in qubit_ids:
        partner = flip_bit(state_pair, qubit_id)
        state_pair = cos_half * state_pair + sin_half * quarter_turn(partner)
    return state_pair


def global_mixer(state_pair, cos_half, sin_half, axis_name, axis_size):
    for bit_id in range(int(math.log2(axis_size))):
        bit_step = 1 << bit_id
        perm_pairs = [(source_id, source_id ^ bit_step) for source_id in range(axis_size)]
        partner = lax.ppermute(state_pair, axis_name, perm_pairs)
        state_pair = cos_half * state_pair + sin_half * quarter_turn(partner)
    return state_pair


def solution(mesh):
    size_x = mesh.shape['qx']
    size_y = mesh.shape['qy']
    state_spec = P(('inst', 'qx', 'qy'))

    def device_body(cost_local, gammas, betas):
        local_len = cost_local.shape[0]
        local_qubits = int(math.log2(local_len))
        row_count = local_len // LANES
        cost_rows = cost_local.reshape(row_count, LANES)
        state_pair = jnp.stack([jnp.ones((row_count, LANES), jnp.float32),
                                jnp.zeros((row_count, LANES), jnp.float32)])
        for layer_id in range(gammas.shape[0]):
            phase_angle = gammas[layer_id] * cost_rows
            state_pair = jnp.cos(phase_angle) * state_pair + jnp.sin(phase_angle) * quarter_turn(state_pair)
            cos_half = jnp.cos(0.5 * betas[layer_id])
            sin_half = jnp.sin(0.5 * betas[layer_id])
            state_pair = local_mixer(state_pair, cos_half, sin_half, range(local_qubits))
            state_pair = global_mixer(state_pair, cos_half, sin_half, 'qy', size_y)
            state_pair = global_mixer(state_pair, cos_half, sin_half, 'qx', size_x)
        local_energy = jnp.sum(cost_rows * (state_pair[0] * state_pair[0] + state_pair[1] * state_pair[1]))
        energy = lax.psum(local_energy, ('qx', 'qy')) / (local_len * size_x * size_y)
        return energy.reshape(1), state_pair[0].reshape(local_len), state_pair[1].reshape(local_len)

    return jax.shard_map(device_body, mesh=mesh, in_specs=(state_spec, P(), P()),
                         out_specs=(P('inst'), state_spec, state_spec), check_vma=False)
```

profile of v0, /device:TPU:0, one launch (start us, length us, event | category | flops | bytes accessed | tf_op | source)
XLA Modules:
  0.0 1152.1 jit_solution(1983174130942036038)
XLA Ops:
  0.6 1.6 fusion.273
  2.2 36.6 %cosine_bitcast_fusion.7 = (f32[2048,128]{1,0:T(8,128)}, f32[2048,128]{1,0:T(8,128)}, f32[2048,128]{1,0:T(8,128)}, f32[2048,128]{1,0:T(8,128)}, f32[2048,128]{1,...) fusion(f32[262144]{0:T(1024)} %param.179, ...), kind=kLoop, calls=%fused_computation.338 | loop fusion | flops 2097152 | bytes 17825824 | tf_op jit(solution)/shard_map/cos | solution.py:61
  42.7 1.1 maximum_select_fusion
  45.9 1.1 maximum_select_fusion.1
  49.4 1.1 maximum_select_fusion.2
  52.3 1.5 maximum_select_fusion.3
  55.5 1.1 maximum_select_fusion.4
  76.9 3.4 collective-permute-start
  80.3 45.6 %collective-permute-done = f32[2,2048,128]{2,1,0:T(8,128)S(1)} collective-permute-done((f32[2,2048,128]{2,1,0:T(8,128)S(1)}, f32[2,2048,128]{2,1,0:T(8,128)S(1)}, u32[]{:S(2)}, u32[]{:S(2)}) %collective-permute-start) | collective-permute-done | bytes 2097184 | tf_op jit(solution)/shard_map/ppermute | solution.py:42
  126.3 4.1 collective-permute-done.1
  130.8 1.7 collective-permute-start.2
  133.3 45.2 %collective-permute-done.2 = f32[2,2048,128]{2,1,0:T(8,128)S(1)} collective-permute-done((f32[2,2048,128]{2,1,0:T(8,128)S(1)}, f32[2,2048,128]{2,1,0:T(8,128)S(1)}, u32[]{:S(2)}, u32[]{:S(2)}) %collective-permute-start.2) | collective-permute-done | bytes 2097184 | tf_op jit(solution)/shard_map/ppermute | solution.py:42
  202.4 1.4 maximum_select_fusion.24
  214.3 1.8 collective-permute-start.3
  216.0 45.1 %collective-permute-done.3 = f32[2,2048,128]{2,1,0:T(8,128)S(1)} collective-permute-done((f32[2,2048,128]{2,1,0:T(8,128)S(1)}, f32[2,2048,128]{2,1,0:T(8,128)S(1)}, u32[]{:S(2)}, u32[]{:S(2)}) %collective-permute-start.3) | collective-permute-done | bytes 2097184 | tf_op jit(solution)/shard_map/ppermute | solution.py:42
  261.5 4.1 collective-permute-done.4
  266.0 1.7 collective-permute-start.5
  268.4 45.2 %collective-permute-done.5 = f32[2,2048,128]{2,1,0:T(8,128)S(1)} collective-permute-done((f32[2,2048,128]{2,1,0:T(8,128)S(1)}, f32[2,2048,128]{2,1,0:T(8,128)S(1)}, u32[]{:S(2)}, u32[]{:S(2)}) %collective-permute-start.5) | collective-permute-done | bytes 2097184 | tf_op jit(solution)/shard_map/ppermute | solution.py:42
  315.8 1.1 maximum_select_fusion.32
  337.4 1.4 maximum_select_fusion.40
  349.3 1.8 collective-permute-start.6
  351.1 45.1 %collective-permute-done.6 = f32[2,2048,128]{2,1,0:T(8,128)S(1)} collective-permute-done((f32[2,2048,128]{2,1,0:T(8,128)S(1)}, f32[2,2048,128]{2,1,0:T(8,128)S(1)}, u32[]{:S(2)}, u32[]{:S(2)}) %collective-permute-start.6) | collective-permute-done | bytes 2097184 | tf_op jit(solution)/shard_map/ppermute | solution.py:42
  396.6 4.1 collective-permute-done.7
  401.1 1.7 collective-permute-start.8
  403.6 45.2 %collective-permute-done.8 = f32[2,2048,128]{2,1,0:T(8,128)S(1)} collective-permute-done((f32[2,2048,128]{2,1,0:T(8,128)S(1)}, f32[2,2048,128]{2,1,0:T(8,128)S(1)}, u32[]{:S(2)}, u32[]{:S(2)}) %collective-permute-start.8) | collective-permute-done | bytes 2097184 | tf_op jit(solution)/shard_map/ppermute | solution.py:42
  450.9 1.1 maximum_select_fusion.48
  472.5 1.4 maximum_select_fusion.56
  484.4 1.8 collective-permute-start.9
  486.2 45.1 %collective-permute-done.9 = f32[2,2048,128]{2,1,0:T(8,128)S(1)} collective-permute-done((f32[2,2048,128]{2,1,0:T(8,128)S(1)}, f32[2,2048,128]{2,1,0:T(8,128)S(1)}, u32[]{:S(2)}, u32[]{:S(2)}) %collective-permute-start.9) | collective-permute-done | bytes 2097184 | tf_op jit(solution)/shard_map/ppermute | solution.py:42
  531.6 4.1 collective-permute-done.10
  536.1 1.7 collective-permute-start.11
  538.6 45.2 %collective-permute-done.11 = f32[2,2048,128]{2,1,0:T(8,128)S(1)} collective-permute-done((f32[2,2048,128]{2,1,0:T(8,128)S(1)}, f32[2,2048,128]{2,1,0:T(8,128)S(1)}, u32[]{:S(2)}, u32[]{:S(2)}) %collective-permute-start.11) | collective-permute-done | bytes 2097184 | tf_op jit(solution)/shard_map/ppermute | solution.py:42
  585.9 1.1 maximum_select_fusion.64
  607.5 1.4 maximum_select_fusion.72
  619.5 1.8 collective-permute-start.12
  621.2 45.1 %collective-permute-done.12 = f32[2,2048,128]{2,1,0:T(8,128)S(1)} collective-permute-done((f32[2,2048,128]{2,1,0:T(8,128)S(1)}, f32[2,2048,128]{2,1,0:T(8,128)S(1)}, u32[]{:S(2)}, u32[]{:S(2)}) %collective-permute-start.12) | collective-permute-done | bytes 2097184 | tf_op jit(solution)/shard_map/ppermute | solution.py:42
  666.7 4.1 collective-permute-done.13
  671.2 1.7 collective-permute-start.14
  673.7 45.2 %collective-permute-done.14 = f32[2,2048,128]{2,1,0:T(8,128)S(1)} collective-permute-done((f32[2,2048,128]{2,1,0:T(8,128)S(1)}, f32[2,2048,128]{2,1,0:T(8,128)S(1)}, u32[]{:S(2)}, u32[]{:S(2)}) %collective-permute-start.14) | collective-permute-done | bytes 2097184 | tf_op jit(solution)/shard_map/ppermute | solution.py:42
  721.0 1.1 maximum_select_fusion.80
  726.9 1.1 maximum_select_fusion.82
  730.0 1.1 maximum_select_fusion.83
  742.6 1.4 maximum_select_fusion.88
  754.5 1.8 collective-permute-start.15
  756.3 45.1 %collective-permute-done.15 = f32[2,2048,128]{2,1,0:T(8,128)S(1)} collective-permute-done((f32[2,2048,128]{2,1,0:T(8,128)S(1)}, f32[2,2048,128]{2,1,0:T(8,128)S(1)}, u32[]{:S(2)}, u32[]{:S(2)}) %collective-permute-start.15) | collective-permute-done | bytes 2097184 | tf_op jit(solution)/shard_map/ppermute | solution.py:42
  801.7 4.1 collective-permute-done.16
  806.2 1.7 collective-permute-start.17
  808.8 45.2 %collective-permute-done.17 = f32[2,2048,128]{2,1,0:T(8,128)S(1)} collective-permute-done((f32[2,2048,128]{2,1,0:T(8,128)S(1)}, f32[2,2048,128]{2,1,0:T(8,128)S(1)}, u32[]{:S(2)}, u32[]{:S(2)}) %collective-permute-start.17) | collective-permute-done | bytes 2097184 | tf_op jit(solution)/shard_map/ppermute | solution.py:42
  856.1 1.1 maximum_select_fusion.96
  877.7 1.4 maximum_select_fusion.104
  889.6 1.8 collective-permute-start.18
  891.3 45.1 %collective-permute-done.18 = f32[2,2048,128]{2,1,0:T(8,128)S(1)} collective-permute-done((f32[2,2048,128]{2,1,0:T(8,128)S(1)}, f32[2,2048,128]{2,1,0:T(8,128)S(1)}, u32[]{:S(2)}, u32[]{:S(2)}) %collective-permute-start.18) | collective-permute-done | bytes 2097184 | tf_op jit(solution)/shard_map/ppermute | solution.py:42
  936.8 4.1 collective-permute-done.19
  941.3 1.7 collective-permute-start.20
  943.9 45.1 %collective-permute-done.20 = f32[2,2048,128]{2,1,0:T(8,128)S(1)} collective-permute-done((f32[2,2048,128]{2,1,0:T(8,128)S(1)}, f32[2,2048,128]{2,1,0:T(8,128)S(1)}, u32[]{:S(2)}, u32[]{:S(2)}) %collective-permute-start.20) | collective-permute-done | bytes 2097184 | tf_op jit(solution)/shard_map/ppermute | solution.py:42
  991.1 1.1 maximum_select_fusion.112
  1012.7 1.3 maximum_select_fusion.120
  1024.3 1.8 collective-permute-start.21
  1026.1 45.1 %collective-permute-done.21 = f32[2,2048,128]{2,1,0:T(8,128)S(1)} collective-permute-done((f32[2,2048,128]{2,1,0:T(8,128)S(1)}, f32[2,2048,128]{2,1,0:T(8,128)S(1)}, u32[]{:S(2)}, u32[]{:S(2)}) %collective-permute-start.21) | collective-permute-done | bytes 2097184 | tf_op jit(solution)/shard_map/ppermute | solution.py:42
  1071.5 4.1 collective-permute-done.22
  1076.1 1.7 collective-permute-start.23
  1077.8 46.0 %collective-permute-done.23 = f32[2,2048,128]{2,1,0:T(8,128)S(1)} collective-permute-done((f32[2,2048,128]{2,1,0:T(8,128)S(1)}, f32[2,2048,128]{2,1,0:T(8,128)S(1)}, u32[]{:S(2)}, u32[]{:S(2)}) %collective-permute-start.23) | collective-permute-done | bytes 2097184 | tf_op jit(solution)/shard_map/ppermute | solution.py:42
  1124.1 2.1 multiply_reduce_fusion
  1126.3 23.6 %psum.7 = f32[]{:T(128)} all-reduce(f32[]{:T(128)} %get-tuple-element.3), channel_id=1, replica_groups=mesh['inst'=1,'qy'=2,'qx'=4] {'qx','qy'}, use_global_device_ids=true, to_apply=%region_1.2 | all-reduce | flops 1 | bytes 8 | tf_op jit(solution)/shard_map/psum | solution.py:68
  (630 shorter events, 263.7 us)
Async XLA Ops:
  2.2 36.6 %copy-start.15 = (f32[2]{0:T(128)S(1)}, f32[2]{0:T(128)}, u32[]{:S(2)}) copy-start(f32[2]{0:T(128)} %constant.17.clone.1) | copy-start | bytes 28
  38.9 0.7 copy-start
  40.6 0.7 copy-start.14
  76.9 49.0 %collective-permute-start = (f32[2,2048,128]{2,1,0:T(8,128)S(1)}, f32[2,2048,128]{2,1,0:T(8,128)S(1)}, u32[]{:S(2)}, u32[]{:S(2)}) collective-permute-start(f32[2,2048,128]{2,1,0:T(8,128)S(1)} %multiply_add_fusion.157), channel_id=1, source_target_pairs={{0,4},{4,0},{1,5},{5,1},{2,6},{6,2},{3,7},{7,3}} | collective-permute-start | bytes 6291464 | tf_op jit(solution)/shard_map/ppermute | solution.py:42
  126.3 4.2 collective-permute-start.1
  130.8 47.7 %collective-permute-start.2 = (f32[2,2048,128]{2,1,0:T(8,128)S(1)}, f32[2,2048,128]{2,1,0:T(8,128)S(1)}, u32[]{:S(2)}, u32[]{:S(2)}) collective-permute-start(f32[2,2048,128]{2,1,0:T(8,128)S(1)} %multiply_add_fusion.155), channel_id=1, source_target_pairs={{0,2},{1,3},{2,0},{3,1},{4,6},{5,7},{6,4},{7,5}} | collective-permute-start | bytes 6291464 | tf_op jit(solution)/shard_map/ppermute | solution.py:42
  214.3 46.8 %collective-permute-start.3 = (f32[2,2048,128]{2,1,0:T(8,128)S(1)}, f32[2,2048,128]{2,1,0:T(8,128)S(1)}, u32[]{:S(2)}, u32[]{:S(2)}) collective-permute-start(f32[2,2048,128]{2,1,0:T(8,128)S(1)} %multiply_add_fusion.135), channel_id=1, source_target_pairs={{0,4},{4,0},{1,5},{5,1},{2,6},{6,2},{3,7},{7,3}} | collective-permute-start | bytes 6291464 | tf_op jit(solution)/shard_map/ppermute | solution.py:42
  261.5 4.2 collective-permute-start.4
  266.0 47.7 %collective-permute-start.5 = (f32[2,2048,128]{2,1,0:T(8,128)S(1)}, f32[2,2048,128]{2,1,0:T(8,128)S(1)}, u32[]{:S(2)}, u32[]{:S(2)}) collective-permute-start(f32[2,2048,128]{2,1,0:T(8,128)S(1)} %multiply_add_fusion.133), channel_id=1, source_target_pairs={{0,2},{1,3},{2,0},{3,1},{4,6},{5,7},{6,4},{7,5}} | collective-permute-start | bytes 6291464 | tf_op jit(solution)/shard_map/ppermute | solution.py:42
  268.4 45.6 %copy-start.11 = (f32[2048,128]{1,0:T(8,128)S(1)}, f32[2048,128]{1,0:T(8,128)}, u32[]{:S(2)}) copy-start(f32[2048,128]{1,0:T(8,128)} %get-tuple-element.556) | copy-start | bytes 3145732
  268.4 45.6 %copy-start.12 = (f32[2048,128]{1,0:T(8,128)S(1)}, f32[2048,128]{1,0:T(8,128)}, u32[]{:S(2)}) copy-start(f32[2048,128]{1,0:T(8,128)} %get-tuple-element.560) | copy-start | bytes 3145732
  349.3 46.8 %collective-permute-start.6 = (f32[2,2048,128]{2,1,0:T(8,128)S(1)}, f32[2,2048,128]{2,1,0:T(8,128)S(1)}, u32[]{:S(2)}, u32[]{:S(2)}) collective-permute-start(f32[2,2048,128]{2,1,0:T(8,128)S(1)} %multiply_add_fusion.113), channel_id=1, source_target_pairs={{0,4},{4,0},{1,5},{5,1},{2,6},{6,2},{3,7},{7,3}} | collective-permute-start | bytes 6291464 | tf_op jit(solution)/shard_map/ppermute | solution.py:42
  396.5 4.2 collective-permute-start.7
  401.1 47.7 %collective-permute-start.8 = (f32[2,2048,128]{2,1,0:T(8,128)S(1)}, f32[2,2048,128]{2,1,0:T(8,128)S(1)}, u32[]{:S(2)}, u32[]{:S(2)}) collective-permute-start(f32[2,2048,128]{2,1,0:T(8,128)S(1)} %multiply_add_fusion.111), channel_id=1, source_target_pairs={{0,2},{1,3},{2,0},{3,1},{4,6},{5,7},{6,4},{7,5}} | collective-permute-start | bytes 6291464 | tf_op jit(solution)/shard_map/ppermute | solution.py:42
  403.6 45.5 %copy-start.9 = (f32[2048,128]{1,0:T(8,128)S(1)}, f32[2048,128]{1,0:T(8,128)}, u32[]{:S(2)}) copy-start(f32[2048,128]{1,0:T(8,128)} %get-tuple-element.555) | copy-start | bytes 3145732
  403.6 45.5 %copy-start.10 = (f32[2048,128]{1,0:T(8,128)S(1)}, f32[2048,128]{1,0:T(8,128)}, u32[]{:S(2)}) copy-start(f32[2048,128]{1,0:T(8,128)} %get-tuple-element.561) | copy-start | bytes 3145732
  484.4 46.8 %collective-permute-start.9 = (f32[2,2048,128]{2,1,0:T(8,128)S(1)}, f32[2,2048,128]{2,1,0:T(8,128)S(1)}, u32[]{:S(2)}, u32[]{:S(2)}) collective-permute-start(f32[2,2048,128]{2,1,0:T(8,128)S(1)} %multiply_add_fusion.91), channel_id=1, source_target_pairs={{0,4},{4,0},{1,5},{5,1},{2,6},{6,2},{3,7},{7,3}} | collective-permute-start | bytes 6291464 | tf_op jit(solution)/shard_map/ppermute | solution.py:42
  531.6 4.2 collective-permute-start.10
  536.1 47.7 %collective-permute-start.11 = (f32[2,2048,128]{2,1,0:T(8,128)S(1)}, f32[2,2048,128]{2,1,0:T(8,128)S(1)}, u32[]{:S(2)}, u32[]{:S(2)}) collective-permute-start(f32[2,2048,128]{2,1,0:T(8,128)S(1)} %multiply_add_fusion.89), channel_id=1, source_target_pairs={{0,2},{1,3},{2,0},{3,1},{4,6},{5,7},{6,4},{7,5}} | collective-permute-start | bytes 6291464 | tf_op jit(solution)/shard_map/ppermute | solution.py:42
  538.6 45.6 %copy-start.7 = (f32[2048,128]{1,0:T(8,128)S(1)}, f32[2048,128]{1,0:T(8,128)}, u32[]{:S(2)}) copy-start(f32[2048,128]{1,0:T(8,128)} %get-tuple-element.554) | copy-start | bytes 3145732
  538.6 45.6 %copy-start.8 = (f32[2048,128]{1,0:T(8,128)S(1)}, f32[2048,128]{1,0:T(8,128)}, u32[]{:S(2)}) copy-start(f32[2048,128]{1,0:T(8,128)} %get-tuple-element.562) | copy-start | bytes 3145732
  619.5 46.8 %collective-permute-start.12 = (f32[2,2048,128]{2,1,0:T(8,128)S(1)}, f32[2,2048,128]{2,1,0:T(8,128)S(1)}, u32[]{:S(2)}, u32[]{:S(2)}) collective-permute-start(f32[2,2048,128]{2,1,0:T(8,128)S(1)} %multiply_add_fusion.69), channel_id=1, source_target_pairs={{0,4},{4,0},{1,5},{5,1},{2,6},{6,2},{3,7},{7,3}} | collective-permute-start | bytes 6291464 | tf_op jit(solution)/shard_map/ppermute | solution.py:42
  666.6 4.2 collective-permute-start.13
  671.2 47.7 %collective-permute-start.14 = (f32[2,2048,128]{2,1,0:T(8,128)S(1)}, f32[2,2048,128]{2,1,0:T(8,128)S(1)}, u32[]{:S(2)}, u32[]{:S(2)}) collective-permute-start(f32[2,2048,128]{2,1,0:T(8,128)S(1)} %multiply_add_fusion.67), channel_id=1, source_target_pairs={{0,2},{1,3},{2,0},{3,1},{4,6},{5,7},{6,4},{7,5}} | collective-permute-start | bytes 6291464 | tf_op jit(solution)/shard_map/ppermute | solution.py:42
  673.7 45.5 %copy-start.5 = (f32[2048,128]{1,0:T(8,128)S(1)}, f32[2048,128]{1,0:T(8,128)}, u32[]{:S(2)}) copy-start(f32[2048,128]{1,0:T(8,128)} %get-tuple-element.553) | copy-start | bytes 3145732
  673.7 45.5 %copy-start.6 = (f32[2048,128]{1,0:T(8,128)S(1)}, f32[2048,128]{1,0:T(8,128)}, u32[]{:S(2)}) copy-start(f32[2048,128]{1,0:T(8,128)} %get-tuple-element.563) | copy-start | bytes 3145732
  754.5 46.8 %collective-permute-start.15 = (f32[2,2048,128]{2,1,0:T(8,128)S(1)}, f32[2,2048,128]{2,1,0:T(8,128)S(1)}, u32[]{:S(2)}, u32[]{:S(2)}) collective-permute-start(f32[2,2048,128]{2,1,0:T(8,128)S(1)} %multiply_add_fusion.47), channel_id=1, source_target_pairs={{0,4},{4,0},{1,5},{5,1},{2,6},{6,2},{3,7},{7,3}} | collective-permute-start | bytes 6291464 | tf_op jit(solution)/shard_map/ppermute | solution.py:42
  801.7 4.2 collective-permute-start.16
  806.2 47.7 %collective-permute-start.17 = (f32[2,2048,128]{2,1,0:T(8,128)S(1)}, f32[2,2048,128]{2,1,0:T(8,128)S(1)}, u32[]{:S(2)}, u32[]{:S(2)}) collective-permute-start(f32[2,2048,128]{2,1,0:T(8,128)S(1)} %multiply_add_fusion.45), channel_id=1, source_target_pairs={{0,2},{1,3},{2,0},{3,1},{4,6},{5,7},{6,4},{7,5}} | collective-permute-start | bytes 6291464 | tf_op jit(solution)/shard_map/ppermute | solution.py:42
  808.8 45.5 %copy-start.3 = (f32[2048,128]{1,0:T(8,128)S(1)}, f32[2048,128]{1,0:T(8,128)}, u32[]{:S(2)}) copy-start(f32[2048,128]{1,0:T(8,128)} %get-tuple-element.552) | copy-start | bytes 3145732
  808.8 45.5 %copy-start.4 = (f32[2048,128]{1,0:T(8,128)S(1)}, f32[2048,128]{1,0:T(8,128)}, u32[]{:S(2)}) copy-start(f32[2048,128]{1,0:T(8,128)} %get-tuple-element.564) | copy-start | bytes 3145732
  889.6 46.8 %collective-permute-start.18 = (f32[2,2048,128]{2,1,0:T(8,128)S(1)}, f32[2,2048,128]{2,1,0:T(8,128)S(1)}, u32[]{:S(2)}, u32[]{:S(2)}) collective-permute-start(f32[2,2048,128]{2,1,0:T(8,128)S(1)} %multiply_add_fusion.25), channel_id=1, source_target_pairs={{0,4},{4,0},{1,5},{5,1},{2,6},{6,2},{3,7},{7,3}} | collective-permute-start | bytes 6291464 | tf_op jit(solution)/shard_map/ppermute | solution.py:42
  936.8 4.2 collective-permute-start.19
  941.3 47.7 %collective-permute-start.20 = (f32[2,2048,128]{2,1,0:T(8,128)S(1)}, f32[2,2048,128]{2,1,0:T(8,128)S(1)}, u32[]{:S(2)}, u32[]{:S(2)}) collective-permute-start(f32[2,2048,128]{2,1,0:T(8,128)S(1)} %multiply_add_fusion.23), channel_id=1, source_target_pairs={{0,2},{1,3},{2,0},{3,1},{4,6},{5,7},{6,4},{7,5}} | collective-permute-start | bytes 6291464 | tf_op jit(solution)/shard_map/ppermute | solution.py:42
  943.8 45.5 %copy-start.1 = (f32[2048,128]{1,0:T(8,128)S(1)}, f32[2048,128]{1,0:T(8,128)}, u32[]{:S(2)}) copy-start(f32[2048,128]{1,0:T(8,128)} %get-tuple-element.550) | copy-start | bytes 3145732
  943.9 45.5 %copy-start.2 = (f32[2048,128]{1,0:T(8,128)S(1)}, f32[2048,128]{1,0:T(8,128)}, u32[]{:S(2)}) copy-start(f32[2048,128]{1,0:T(8,128)} %get-tuple-element.551) | copy-start | bytes 3145732
  1024.3 46.8 %collective-permute-start.21 = (f32[2,2048,128]{2,1,0:T(8,128)S(1)}, f32[2,2048,128]{2,1,0:T(8,128)S(1)}, u32[]{:S(2)}, u32[]{:S(2)}) collective-permute-start(f32[2,2048,128]{2,1,0:T(8,128)S(1)} %multiply_add_fusion.3), channel_id=1, source_target_pairs={{0,4},{4,0},{1,5},{5,1},{2,6},{6,2},{3,7},{7,3}} | collective-permute-start | bytes 6291464 | tf_op jit(solution)/shard_map/ppermute | solution.py:42
  1071.5 4.2 collective-permute-start.22
  1076.0 48.1 %copy-start.13 = (f32[262144]{0:T(1024)S(1)}, f32[262144]{0:T(1024)}, u32[]{:S(2)}) copy-start(f32[262144]{0:T(1024)} %param.179) | copy-start | bytes 3145732
  1076.1 47.7 %collective-permute-start.23 = (f32[2,2048,128]{2,1,0:T(8,128)S(1)}, f32[2,2048,128]{2,1,0:T(8,128)S(1)}, u32[]{:S(2)}, u32[]{:S(2)}) collective-permute-start(f32[2,2048,128]{2,1,0:T(8,128)S(1)} %multiply_add_fusion.1), channel_id=1, source_target_pairs={{0,2},{1,3},{2,0},{3,1},{4,6},{5,7},{6,4},{7,5}} | collective-permute-start | bytes 6291464 | tf_op jit(solution)/shard_map/ppermute | solution.py:42
where the time goes:
time: 1160 us; the launch traced here: 1150 us
  waiting for transfers between devices  757 us (65%)
  other arithmetic  232 us (20%)
  local copies, waits for them, and re-layouts  96.7 us (8%)
  starting transfers between devices  29.8 us (3%)
  blocking collectives  23.6 us (2%)
  between operations  13.1 us (1%)
    ppermute x24, waiting for transfers between devices, global_mixer(): partner = lax.ppermute(state_pair, axis_name, perm_pairs)  757 us
    select_n x128, other arithmetic, flip_bit(): jnp.where(bit_set, jnp.roll(state_pair, bit_step, axis=axis_id), jnp.roll...  121 us
    slice x256, local copies, waits for them, and re-layouts, flip_bit(): jnp.roll(state_pair, -bit_step, axis=axis_id)  87.3 us
    add x144, other arithmetic, local_mixer(): state_pair = cos_half * state_pair + sin_half * quarter_turn(partner)  54.8 us
    cos x1, other arithmetic, device_body(): jnp.cos(phase_angle) * state_pair  36.6 us
    ppermute x24, starting transfers between devices, global_mixer(): partner = lax.ppermute(state_pair, axis_name, perm_pairs)  29.8 us
    psum x1, blocking collectives, device_body(): lax.psum(local_energy, ('qx', 'qy')) / (local_len * size_x * size_y)  23.6 us
  transfers between devices with their start and end apart: 24, of which 24 were waited for; matrix products, arithmetic and copies ran while one was open for 0% of the time, Pallas kernels for 0%

commit v1 on v0

v1 whole, which is shorter than its diff:
```python
import functools
import jax
import jax.numpy as jnp
from jax import lax
from jax.experimental import pallas as pl
from jax.experimental.pallas import tpu as pltpu
from jax.sharding import PartitionSpec as P

LANES = 128
LAYERS = 8
HIGH = (8, 4)
LOW = (4, 8)


def rotate(re, im, cos_half, sin_half):
    count = len(re)
    step = 1
    while step < count:
        new_re = [cos_half * re[i] + sin_half * im[i ^ step] for i in range(count)]
        new_im = [cos_half * im[i] - sin_half * re[i ^ step] for i in range(count)]
        re, im = new_re, new_im
        step *= 2
    return re, im


def sublane_rotate(re, im, cos_half, sin_half):
    row = lax.broadcasted_iota(jnp.int32, (8, LANES), 0)
    for step in (1, 2, 4):
        bit_set = (row & step) != 0

        def flip(value):
            down = pltpu.roll(value, step, 0)
            if step == 4:
                return down
            return jnp.where(bit_set, down, pltpu.roll(value, 8 - step, 0))

        flip_re = [flip(value) for value in re]
        flip_im = [flip(value) for value in im]
        re, im = ([cos_half * r + sin_half * fi for r, fi in zip(re, flip_im)],
                  [cos_half * i - sin_half * fr for i, fr in zip(im, flip_re)])
    return re, im


def lane_matrix(cos_half, sin_half):
    row = lax.broadcasted_iota(jnp.int32, (LANES, LANES), 0)
    col = lax.broadcasted_iota(jnp.int32, (LANES, LANES), 1)
    diff = row ^ col
    cos_full = jnp.broadcast_to(cos_half[0:1], (LANES, LANES))
    sin_full = jnp.broadcast_to(sin_half[0:1], (LANES, LANES))
    mag = jnp.ones((LANES, LANES), jnp.float32)
    weight = jnp.zeros((LANES, LANES), jnp.int32)
    for bit in range(7):
        on = (diff >> bit) & 1
        mag = mag * jnp.where(on == 1, sin_full, cos_full)
        weight = weight + on
    quarter = weight & 3
    zero = jnp.zeros_like(mag)
    real = jnp.where(quarter == 0, mag, jnp.where(quarter == 2, -mag, zero))
    imag = jnp.where(quarter == 1, -mag, jnp.where(quarter == 3, mag, zero))
    return real, imag


def kernel(cost, gammas, betas, energy, out_re, out_im,
           cost_swap, recv_high, recv_low, send_high, send_low, work, cos_buf, sin_buf,
           rows_in, rows_out, matrix, energy_part, energy_all,
           cost_send, cost_recv, high_send, high_recv, low_send, low_recv, e_send, e_recv):
    qx = lax.axis_index('qx')
    qy = lax.axis_index('qy')
    bits = (qy, qx % 2, qx // 2)

    def flipped(offset):
        return [1 - bit if (offset >> i) & 1 else bit for i, bit in enumerate(bits)]

    def block(offset):
        y, core, x = flipped(offset)
        return (x * 2 + core) * 2 + y

    def peer(offset):
        y, core, x = flipped(offset)
        return {'qy': y, 'qx': x * 2 + core}

    barrier = pltpu.get_barrier_semaphore()
    for offset in range(1, 8):
        pl.semaphore_signal(barrier, inc=1, device_id=peer(offset), device_id_type=pl.DeviceIdType.MESH)
    pl.semaphore_wait(barrier, 7)

    for offset in range(1, 8):
        pltpu.make_async_remote_copy(
            src_ref=cost.at[block(offset)], dst_ref=cost_swap.at[offset],
            send_sem=cost_send, recv_sem=cost_recv,
            device_id=peer(offset), device_id_type=pl.DeviceIdType.MESH).start()

    def half_angle(layer):
        angle = jnp.full((8, LANES), 0.5 * betas[layer], jnp.float32)
        return jnp.cos(angle), jnp.sin(angle)

    def group(split, chunk, j):
        if split is HIGH:
            return pl.multiple_of((chunk * 4 + j) * 8, 8)
        return pl.multiple_of((j * 4 + chunk) * 8, 8)

    def cost_rows(swapped, offset, start):
        if swapped:
            return cost_swap[offset, pl.ds(start, 8), :]
        return cost[block(offset), pl.ds(start, 8), :]

    def trig(layer, split, swapped, chunk):
        gamma = gammas[layer]

        def body(j, carry):
            start = group(split, chunk, j)
            row = pl.multiple_of(j * 8, 8)
            for offset in range(8):
                angle = gamma * cost_rows(swapped, offset, start)
                cos_buf[offset, pl.ds(row, 8), :] = jnp.cos(angle)
                sin_buf[offset, pl.ds(row, 8), :] = jnp.sin(angle)
            return carry

        lax.fori_loop(0, split[1], body, 0)

    def wait_all(buffer, sem, chunk):
        part = buffer.at[chunk, pl.ds(1, 7)]
        pltpu.make_async_copy(part, part, sem.at[chunk]).wait()

    def layer_step(layer, split, first):
        swapped = split is HIGH
        if swapped:
            recv, recv_sem, send, send_sem, target, target_sem, out_split = (
                recv_high, high_recv, send_low, low_send, recv_low, low_recv, LOW)
        else:
            recv, recv_sem, send, send_sem, target, target_sem, out_split = (
                recv_low, low_recv, send_high, high_send, recv_high, high_recv, HIGH)
        chunks, per_slot = split
        cos_half, sin_half = half_angle(layer)
        if not first:
            cos_prev, sin_prev = half_angle(layer - 1)
        real, imag = lane_matrix(cos_half, sin_half)
        matrix[0:LANES, 0:LANES] = real
        matrix[0:LANES, LANES:] = imag
        matrix[LANES:, 0:LANES] = -imag
        matrix[LANES:, LANES:] = real

        def in_chunk(chunk, carry):
            trig(layer, split, swapped, chunk)
            if not first:
                wait_all(recv, recv_sem, chunk)

            def slots(j, carry):
                row = pl.multiple_of(j * 8, 8)
                cos_phase = [cos_buf[o, pl.ds(row, 8), :] for o in range(8)]
                sin_phase = [sin_buf[o, pl.ds(row, 8), :] for o in range(8)]
                if first:
                    re = cos_phase
                    im = [-value for value in sin_phase]
                else:
                    old_re = [recv[chunk, o, 0, pl.ds(row, 8), :] for o in range(8)]
                    old_im = [recv[chunk, o, 1, pl.ds(row, 8), :] for o in range(8)]
                    old_re, old_im = rotate(old_re, old_im, cos_prev, sin_prev)
                    re = [r * c + i * s for r, i, c, s in zip(old_re, old_im, cos_phase, sin_phase)]
                    im = [i * c - r * s for r, i, c, s in zip(old_re, old_im, cos_phase, sin_phase)]
                re, im = rotate(re, im, cos_half, sin_half)
                re, im = sublane_rotate(re, im, cos_half, sin_half)
                for o in range(8):
                    at = pl.multiple_of(o * per_slot * 8 + row, 8)
                    rows_in[pl.ds(at, 8), 0:LANES] = re[o]
                    rows_in[pl.ds(at, 8), LANES:] = im[o]
                return carry

            lax.fori_loop(0, per_slot, slots, 0)
            count = 64 * per_slot
            for base in range(0, count, 256):
                rows_out[base:base + 256, :] = lax.dot(
                    rows_in[base:base + 256, :], matrix[...],
                    precision=lax.Precision.HIGHEST, preferred_element_type=jnp.float32)

            def within(o, carry):
                base = pl.multiple_of(o * per_slot * 8, 8)
                re = [rows_out[pl.ds(base + 8 * j, 8), 0:LANES] for j in range(per_slot)]
                im = [rows_out[pl.ds(base + 8 * j, 8), LANES:] for j in range(per_slot)]
                re, im = rotate(re, im, cos_half, sin_half)
                for j in range(per_slot):
                    start = group(split, chunk, j)
                    work[o, 0, pl.ds(start, 8), :] = re[j]
                    work[o, 1, pl.ds(start, 8), :] = im[j]
                return carry

            lax.fori_loop(0, 8, within, 0)
            return carry

        lax.fori_loop(0, chunks, in_chunk, 0)

        out_chunks, out_per_slot = out_split

        def out_chunk(chunk, carry):
            def across(o, slot_target):
                re = [work[o, 0, pl.ds(group(out_split, chunk, j), 8), :] for j in range(out_per_slot)]
                im = [work[o, 1, pl.ds(group(out_split, chunk, j), 8), :] for j in range(out_per_slot)]
                re, im = rotate(re, im, cos_half, sin_half)
                for j in range(out_per_slot):
                    slot_target[chunk, o, 0, 8 * j:8 * j + 8, :] = re[j]
                    slot_target[chunk, o, 1, 8 * j:8 * j + 8, :] = im[j]

            def body(o, carry):
                across(o, send)
                return carry

            lax.fori_loop(1, 8, body, 0)
            for offset in range(1, 8):
                pltpu.make_async_remote_copy(
                    src_ref=send.at[chunk, offset], dst_ref=target.at[chunk, offset],
                    send_sem=send_sem.at[chunk], recv_sem=target_sem.at[chunk],
                    device_id=peer(offset), device_id_type=pl.DeviceIdType.MESH).start()
            across(0, target)
            return carry

        def drain(chunk, carry):
            wait_all(send, send_sem, chunk)
            return carry

        return out_chunk, drain, out_chunks

    def run_layer(layer, split, first, reuse):
        out_chunk, drain, out_chunks = layer_step(layer, split, first)
        if reuse:
            lax.fori_loop(0, out_chunks, drain, 0)
        lax.fori_loop(0, out_chunks, out_chunk, 0)

    run_layer(0, LOW, True, False)
    cost_swap[0] = cost[block(0)]
    part = cost_swap.at[pl.ds(1, 7)]
    pltpu.make_async_copy(part, part, cost_recv).wait()
    run_layer(1, HIGH, False, False)

    def pair(i, carry):
        run_layer(2 * i + 2, LOW, False, True)
        run_layer(2 * i + 3, HIGH, False, True)
        return carry

    lax.fori_loop(0, LAYERS // 2 - 1, pair, 0)

    cos_half, sin_half = half_angle(LAYERS - 1)
    energy_part[...] = jnp.zeros((8, LANES), jnp.float32)

    def final_chunk(chunk, carry):
        wait_all(recv_low, low_recv, chunk)

        def slots(j, carry):
            row = pl.multiple_of(j * 8, 8)
            start = group(LOW, chunk, j)
            re = [recv_low[chunk, o, 0, pl.ds(row, 8), :] for o in range(8)]
            im = [recv_low[chunk, o, 1, pl.ds(row, 8), :] for o in range(8)]
            re, im = rotate(re, im, cos_half, sin_half)
            total = energy_part[...]
            for o in range(8):
                at = block(o)
                out_re[at, pl.ds(start, 8), :] = re[o]
                out_im[at, pl.ds(start, 8), :] = im[o]
                total = total + cost[at, pl.ds(start, 8), :] * (re[o] * re[o] + im[o] * im[o])
            energy_part[...] = total
            return carry

        lax.fori_loop(0, LOW[1], slots, 0)
        return carry

    lax.fori_loop(0, LOW[0], final_chunk, 0)

    me = block(0)
    for offset in range(1, 8):
        pltpu.make_async_remote_copy(
            src_ref=energy_part, dst_ref=energy_all.at[me],
            send_sem=e_send.at[offset], recv_sem=e_recv.at[offset],
            device_id=peer(offset), device_id_type=pl.DeviceIdType.MESH).start()
    energy_all[me] = energy_part[...]
    for chunk in range(HIGH[0]):
        wait_all(send_high, high_send, chunk)
    for chunk in range(LOW[0]):
        wait_all(send_low, low_send, chunk)
    part = cost.at[pl.ds(1, 7)]
    pltpu.make_async_copy(part, part, cost_send).wait()
    for offset in range(1, 8):
        pltpu.make_async_copy(energy_part, energy_part, e_send.at[offset]).wait()
        pltpu.make_async_copy(energy_part, energy_part, e_recv.at[offset]).wait()
    total = energy_all[0]
    for i in range(1, 8):
        total = total + energy_all[i]
    energy[0] = jnp.sum(total) * (1.0 / (1 << 21))


def solution(mesh):
    state_spec = P(('inst', 'qx', 'qy'))

    def device_body(cost_local, gammas, betas):
        local_len = cost_local.shape[0]
        rows = local_len // (8 * LANES)
        shape = (8, rows, LANES)
        f32 = jnp.float32
        vmem = pl.BlockSpec(memory_space=pltpu.VMEM)
        smem = pl.BlockSpec(memory_space=pltpu.SMEM)
        dma = pltpu.SemaphoreType.DMA
        high = (HIGH[0], 8, 2, 8 * HIGH[1], LANES)
        low = (LOW[0], 8, 2, 8 * LOW[1], LANES)
        energy, state_re, state_im = pl.pallas_call(
            kernel,
            out_shape=(jax.ShapeDtypeStruct((1,), f32),
                       jax.ShapeDtypeStruct(shape, f32), jax.ShapeDtypeStruct(shape, f32)),
            in_specs=[vmem, smem, smem],
            out_specs=(smem, vmem, vmem),
            scratch_shapes=[
                pltpu.VMEM(shape, f32),
                pltpu.VMEM(high, f32), pltpu.VMEM(low, f32),
                pltpu.VMEM(high, f32), pltpu.VMEM(low, f32),
                pltpu.VMEM((8, 2, rows, LANES), f32),
                pltpu.VMEM((8, 8 * LOW[1], LANES), f32), pltpu.VMEM((8, 8 * LOW[1], LANES), f32),
                pltpu.VMEM((64 * LOW[1], 2 * LANES), f32), pltpu.VMEM((64 * LOW[1], 2 * LANES), f32),
                pltpu.VMEM((2 * LANES, 2 * LANES), f32),
                pltpu.VMEM((8, LANES), f32), pltpu.VMEM((8, 8, LANES), f32),
                dma, dma,
                dma((HIGH[0],)), dma((HIGH[0],)), dma((LOW[0],)), dma((LOW[0],)),
                dma((8,)), dma((8,)),
            ],
            compiler_params=pltpu.CompilerParams(collective_id=0, has_side_effects=True),
            name='qaoa',
        )(cost_local.reshape(shape), gammas, betas)
        return energy, state_re.reshape(local_len), state_im.reshape(local_len)

    return jax.shard_map(device_body, mesh=mesh, in_specs=(state_spec, P(), P()),
                         out_specs=(P('inst'), state_spec, state_spec), check_vma=False)
```

time: 1160 us -> 233 us (0.20)
  waiting for transfers between devices: 757 us -> 0 us
  other arithmetic: 232 us -> 0 us
  Pallas kernels: 0 us -> 227 us
  local copies, waits for them, and re-layouts: 96.7 us -> 3.39 us
  starting transfers between devices: 29.8 us -> 0 us
  blocking collectives: 23.6 us -> 0 us
    ppermute x24 -> x0, waiting for transfers between devices: 757 us -> none  [global_mixer(): partner = lax.ppermute(state_pair, axis_name, perm_pairs)]
    pallas_call x0 -> x1, Pallas kernels: none -> 227 us  [device_body(): pl.pallas_call(kernel, out_shape=(jax.ShapeDtypeStruct((1,), f32), jax.Sh...]
    select_n x128 -> x0, other arithmetic: 121 us -> none  [flip_bit(): jnp.where(bit_set, jnp.roll(state_pair, bit_step, axis=axis_id), jnp.roll...]
    slice x274 -> x0, local copies, waits for them, and re-layouts: 95.9 us -> none  [the longest x256 87.3 us: flip_bit(): jnp.roll(state_pair, -bit_step, axis=axis_id)]
    add x176 -> x0, other arithmetic: 66.5 us -> none  [the longest x144 54.8 us: local_mixer(): state_pair = cos_half * state_pair + sin_half * quarter_turn(partner)]
    cos x1 -> x0, other arithmetic: 36.6 us -> none  [device_body(): jnp.cos(phase_angle) * state_pair]
    ppermute x24 -> x0, starting transfers between devices: 29.8 us -> none  [global_mixer(): partner = lax.ppermute(state_pair, axis_name, perm_pairs)]
    psum x1 -> x0, blocking collectives: 23.6 us -> none  [device_body(): lax.psum(local_energy, ('qx', 'qy')) / (local_len * size_x * size_y)]
  transfers between devices with their start and end apart: 24 -> 0, of which waited for: 24 -> 0; matrix products, arithmetic and copies ran while one was open for 0% -> 0% of each run, Pallas kernels for 0% -> 0%
where the time goes in v1:
time: 233 us
  Pallas kernels  227 us (97%)
  local copies, waits for them, and re-layouts  3.39 us (1%)
  between operations  2.39 us (1%)
    pallas_call x1, Pallas kernels, device_body(): pl.pallas_call(kernel, out_shape=(jax.ShapeDtypeStruct((1,), f32), jax.Sh...  227 us

profile of v1, /device:TPU:0, one launch (start us, length us, event | category | flops | bytes accessed | tf_op | source)
XLA Modules:
  0.0 233.0 jit_solution(1818971042021602894)
XLA Ops:
  0.6 227.2 %qaoa.1 = (f32[1]{0:T(128)}, f32[8,256,128]{2,1,0:T(8,128)}, f32[8,256,128]{2,1,0:T(8,128)}) custom-call(f32[8,256,128]{2,1,0:T(8,128)} %bitcast.3, f32[8]{0:T(128)} %gammas.1, f32[8]{0:T(128)} %betas.1), custom_call_target="tpu_custom_call" | custom-call | tf_op jit(solution)/shard_map/qaoa/pallas_call | solution.py:302
  228.5 0.0 copy-start
  228.5 2.4 %copy.10 = f32[262144]{0:T(1024)} copy(f32[262144]{0:T(1024)} %bitcast.5) | data formatting | bytes 2097152
  230.8 0.0 copy-done
  230.8 1.0 copy.11
Async XLA Ops:
  228.5 2.4 %copy-start = (f32[8,256,128]{2,1,0:T(8,128)S(1)}, f32[8,256,128]{2,1,0:T(8,128)}, u32[]{:S(2)}) copy-start(f32[8,256,128]{2,1,0:T(8,128)} %get-tuple-element.8) | copy-start | bytes 3145732

commit v2 on v1

v2 whole, which is shorter than its diff:
```python
import jax
import jax.numpy as jnp
from jax import lax
from jax.experimental import pallas as pl
from jax.experimental.pallas import tpu as pltpu
from jax.sharding import PartitionSpec as P

LANES = 128
LAYERS = 8
SUB = 2
PER_SUB = 8 // SUB


def rotate(re, im, cos_half, sin_half):
    count = len(re)
    step = 1
    while step < count:
        new_re = [cos_half * re[i] + sin_half * im[i ^ step] for i in range(count)]
        new_im = [cos_half * im[i] - sin_half * re[i ^ step] for i in range(count)]
        re, im = new_re, new_im
        step *= 2
    return re, im


def sublane_rotate(re, im, cos_half, sin_half):
    row = lax.broadcasted_iota(jnp.int32, (8, LANES), 0)
    for step in (1, 2, 4):
        bit_set = (row & step) != 0

        def flip(value):
            down = pltpu.roll(value, step, 0)
            if step == 4:
                return down
            return jnp.where(bit_set, down, pltpu.roll(value, 8 - step, 0))

        flip_re = [flip(value) for value in re]
        flip_im = [flip(value) for value in im]
        re, im = ([cos_half * r + sin_half * fi for r, fi in zip(re, flip_im)],
                  [cos_half * i - sin_half * fr for i, fr in zip(im, flip_re)])
    return re, im


def lane_matrix(cos_half, sin_half):
    row = lax.broadcasted_iota(jnp.int32, (LANES, LANES), 0)
    col = lax.broadcasted_iota(jnp.int32, (LANES, LANES), 1)
    diff = row ^ col
    cos_full = jnp.broadcast_to(cos_half[0:1], (LANES, LANES))
    sin_full = jnp.broadcast_to(sin_half[0:1], (LANES, LANES))
    mag = jnp.ones((LANES, LANES), jnp.float32)
    weight = jnp.zeros((LANES, LANES), jnp.int32)
    for bit in range(7):
        on = (diff >> bit) & 1
        mag = mag * jnp.where(on == 1, sin_full, cos_full)
        weight = weight + on
    quarter = weight & 3
    zero = jnp.zeros_like(mag)
    real = jnp.where(quarter == 0, mag, jnp.where(quarter == 2, -mag, zero))
    imag = jnp.where(quarter == 1, -mag, jnp.where(quarter == 3, mag, zero))
    return real, imag


def kernel(cost, gammas, betas, energy, out_re, out_im,
           cost_swap, recv, send, work, cos_buf, sin_buf, rows_in, matrix,
           energy_part, energy_all, cost_send, cost_recv, send_sem, recv_sem, e_send, e_recv):
    qx = lax.axis_index('qx')
    qy = lax.axis_index('qy')
    bits = (qy, qx % 2, qx // 2)

    def flipped(offset):
        return [1 - bit if (offset >> i) & 1 else bit for i, bit in enumerate(bits)]

    def block(offset):
        y, core, x = flipped(offset)
        return (x * 2 + core) * 2 + y

    def peer(offset):
        y, core, x = flipped(offset)
        return {'qy': y, 'qx': x * 2 + core}

    barrier = pltpu.get_barrier_semaphore()
    for offset in range(1, 8):
        pl.semaphore_signal(barrier, inc=1, device_id=peer(offset), device_id_type=pl.DeviceIdType.MESH)
    pl.semaphore_wait(barrier, 7)

    for offset in range(1, 8):
        pltpu.make_async_remote_copy(
            src_ref=cost.at[block(offset)], dst_ref=cost_swap.at[offset],
            send_sem=cost_send, recv_sem=cost_recv,
            device_id=peer(offset), device_id_type=pl.DeviceIdType.MESH).start()

    def half_angle(layer):
        angle = jnp.full((8, LANES), 0.5 * betas[layer], jnp.float32)
        return jnp.cos(angle), jnp.sin(angle)

    def wait_all(buffer, sem, at):
        part = buffer.at[(*at, pl.ds(1, 7))]
        pltpu.make_async_copy(part, part, sem.at[at]).wait()

    def run_layer(layer, odd, first, reuse):
        source, target = (0, 1) if odd else (1, 0)

        def quarter(held, mixed):
            return (held, mixed) if odd else (mixed, held)

        cos_half, sin_half = half_angle(layer)
        if not first:
            cos_prev, sin_prev = half_angle(layer - 1)
        gamma = gammas[layer]
        real, imag = lane_matrix(cos_half, sin_half)
        matrix[0:LANES, 0:LANES] = real
        matrix[0:LANES, LANES:] = imag
        matrix[LANES:, 0:LANES] = -imag
        matrix[LANES:, LANES:] = real

        def half(held, carry):
            def trig(r, carry):
                row = pl.multiple_of(r * 8, 8)
                for mixed in range(2):
                    a, b = quarter(held, mixed)
                    start = pl.multiple_of((a * 16 + b * 8 + r) * 8, 8)
                    for o in range(8):
                        if odd:
                            rows = cost[block(o), pl.ds(start, 8), :]
                        else:
                            rows = cost_swap[o, pl.ds(start, 8), :]
                        angle = gamma * rows
                        cos_buf[mixed * 8 + o, pl.ds(row, 8), :] = jnp.cos(angle)
                        sin_buf[mixed * 8 + o, pl.ds(row, 8), :] = jnp.sin(angle)
                return carry

            lax.fori_loop(0, 8, trig, 0)

            def sub_step(sub, carry):
                if not first:
                    for mixed in range(2):
                        wait_all(recv, recv_sem, (source, *quarter(held, mixed), sub))

                def pair_step(pair, carry):
                    def slots(i, carry):
                        row = pl.multiple_of((sub * PER_SUB + pair * 2 + i) * 8, 8)
                        cos_phase = [cos_buf[o, pl.ds(row, 8), :] for o in range(16)]
                        sin_phase = [sin_buf[o, pl.ds(row, 8), :] for o in range(16)]
                        if first:
                            re = cos_phase
                            im = [-value for value in sin_phase]
                        else:
                            local = pl.multiple_of((pair * 2 + i) * 8, 8)
                            old = [[recv[(source, *quarter(held, mixed), sub, o, c, pl.ds(local, 8))]
                                    for mixed in range(2) for o in range(8)] for c in range(2)]
                            old_re, old_im = rotate(*old, cos_prev, sin_prev)
                            re = [r * c + i * s for r, i, c, s in zip(old_re, old_im, cos_phase, sin_phase)]
                            im = [i * c - r * s for r, i, c, s in zip(old_re, old_im, cos_phase, sin_phase)]
                        re, im = rotate(re, im, cos_half, sin_half)
                        re, im = sublane_rotate(re, im, cos_half, sin_half)
                        for o in range(16):
                            at = pl.multiple_of(o * 16 + i * 8, 8)
                            rows_in[pl.ds(at, 8), 0:LANES] = re[o]
                            rows_in[pl.ds(at, 8), LANES:] = im[o]
                        return carry

                    lax.fori_loop(0, 2, slots, 0)
                    work[sub * (PER_SUB // 2) + pair] = lax.dot(
                        rows_in[...], matrix[...],
                        precision=lax.Precision.HIGHEST, preferred_element_type=jnp.float32)
                    return carry

                lax.fori_loop(0, PER_SUB // 2, pair_step, 0)
                return carry

            lax.fori_loop(0, SUB, sub_step, 0)

            if reuse:
                for mixed in range(2):
                    for sub in range(SUB):
                        wait_all(send, send_sem, (target, *quarter(held, mixed), sub))

            def emit(mixed, carry):
                a, b = quarter(held, mixed)

                def across(o, buffer):
                    def part(r, c):
                        at = pl.multiple_of((mixed * 8 + o) * 16 + (r % 2) * 8, 8)
                        return work[r // 2, pl.ds(at, 8), c * LANES:(c + 1) * LANES]

                    re = [part(r, 0) for r in range(8)]
                    im = [part(r, 1) for r in range(8)]
                    re, im = rotate(re, im, cos_half, sin_half)
                    for r in range(8):
                        row = (r % PER_SUB) * 8
                        buffer[target, a, b, r // PER_SUB, o, 0, row:row + 8, :] = re[r]
                        buffer[target, a, b, r // PER_SUB, o, 1, row:row + 8, :] = im[r]

                def body(o, carry):
                    across(o, send)
                    return carry

                lax.fori_loop(1, 8, body, 0)
                for sub in range(SUB):
                    for offset in range(1, 8):
                        pltpu.make_async_remote_copy(
                            src_ref=send.at[target, a, b, sub, offset],
                            dst_ref=recv.at[target, a, b, sub, offset],
                            send_sem=send_sem.at[target, a, b, sub],
                            recv_sem=recv_sem.at[target, a, b, sub],
                            device_id=peer(offset), device_id_type=pl.DeviceIdType.MESH).start()
                across(0, recv)
                return carry

            lax.fori_loop(0, 2, emit, 0)
            return carry

        lax.fori_loop(0, 2, half, 0)

    run_layer(0, True, True, False)
    cost_swap[0] = cost[block(0)]
    part = cost_swap.at[pl.ds(1, 7)]
    pltpu.make_async_copy(part, part, cost_recv).wait()
    run_layer(1, False, False, False)

    def layer_pair(i, carry):
        run_layer(2 * i + 2, True, False, True)
        run_layer(2 * i + 3, False, False, True)
        return carry

    lax.fori_loop(0, LAYERS // 2 - 1, layer_pair, 0)

    cos_half, sin_half = half_angle(LAYERS - 1)
    energy_part[...] = jnp.zeros((8, LANES), jnp.float32)

    def final_half(a, carry):
        def final_sub(sub, carry):
            for b in range(2):
                wait_all(recv, recv_sem, (0, a, b, sub))

            def slots(i, carry):
                row = pl.multiple_of(i * 8, 8)
                old = [[recv[0, a, b, sub, o, c, pl.ds(row, 8), :] for b in range(2) for o in range(8)]
                       for c in range(2)]
                re, im = rotate(*old, cos_half, sin_half)
                total = energy_part[...]
                for b in range(2):
                    start = pl.multiple_of((a * 16 + b * 8 + sub * PER_SUB + i) * 8, 8)
                    for o in range(8):
                        at = block(o)
                        r, m = re[b * 8 + o], im[b * 8 + o]
                        out_re[at, pl.ds(start, 8), :] = r
                        out_im[at, pl.ds(start, 8), :] = m
                        total = total + cost[at, pl.ds(start, 8), :] * (r * r + m * m)
                energy_part[...] = total
                return carry

            lax.fori_loop(0, PER_SUB, slots, 0)
            return carry

        lax.fori_loop(0, SUB, final_sub, 0)
        return carry

    lax.fori_loop(0, 2, final_half, 0)

    me = block(0)
    for offset in range(1, 8):
        pltpu.make_async_remote_copy(
            src_ref=energy_part, dst_ref=energy_all.at[me],
            send_sem=e_send.at[offset], recv_sem=e_recv.at[offset],
            device_id=peer(offset), device_id_type=pl.DeviceIdType.MESH).start()
    energy_all[me] = energy_part[...]
    for par in range(2):
        for a in range(2):
            for b in range(2):
                for sub in range(SUB):
                    wait_all(send, send_sem, (par, a, b, sub))
    part = cost.at[pl.ds(1, 7)]
    pltpu.make_async_copy(part, part, cost_send).wait()
    for offset in range(1, 8):
        pltpu.make_async_copy(energy_part, energy_part, e_send.at[offset]).wait()
        pltpu.make_async_copy(energy_part, energy_part, e_recv.at[offset]).wait()
    total = energy_all[0]
    for i in range(1, 8):
        total = total + energy_all[i]
    energy[0] = jnp.sum(total) * (1.0 / (1 << 21))


def solution(mesh):
    state_spec = P(('inst', 'qx', 'qy'))

    def device_body(cost_local, gammas, betas):
        local_len = cost_local.shape[0]
        rows = local_len // (8 * LANES)
        shape = (8, rows, LANES)
        f32 = jnp.float32
        vmem = pl.BlockSpec(memory_space=pltpu.VMEM)
        smem = pl.BlockSpec(memory_space=pltpu.SMEM)
        dma = pltpu.SemaphoreType.DMA
        parts = (2, 2, 2, SUB, 8, 2, 8 * PER_SUB, LANES)
        energy, state_re, state_im = pl.pallas_call(
            kernel,
            out_shape=(jax.ShapeDtypeStruct((1,), f32),
                       jax.ShapeDtypeStruct(shape, f32), jax.ShapeDtypeStruct(shape, f32)),
            in_specs=[vmem, smem, smem],
            out_specs=(smem, vmem, vmem),
            scratch_shapes=[
                pltpu.VMEM(shape, f32),
                pltpu.VMEM(parts, f32), pltpu.VMEM(parts, f32),
                pltpu.VMEM((4, 2 * LANES, 2 * LANES), f32),
                pltpu.VMEM((16, 64, LANES), f32), pltpu.VMEM((16, 64, LANES), f32),
                pltpu.VMEM((2 * LANES, 2 * LANES), f32), pltpu.VMEM((2 * LANES, 2 * LANES), f32),
                pltpu.VMEM((8, LANES), f32), pltpu.VMEM((8, 8, LANES), f32),
                dma, dma,
                dma((2, 2, 2, SUB)), dma((2, 2, 2, SUB)),
                dma((8,)), dma((8,)),
            ],
            compiler_params=pltpu.CompilerParams(collective_id=0, has_side_effects=True),
            name='qaoa',
        )(cost_local.reshape(shape), gammas, betas)
        return energy, state_re.reshape(local_len), state_im.reshape(local_len)

    return jax.shard_map(device_body, mesh=mesh, in_specs=(state_spec, P(), P()),
                         out_specs=(P('inst'), state_spec, state_spec), check_vma=False)
```

time: 233 us -> 210 us (0.901)
  Pallas kernels: 227 us -> 204 us
    pallas_call x1, Pallas kernels: 227 us -> 204 us  [device_body(): pl.pallas_call(kernel, out_shape=(jax.ShapeDtypeStruct((1,), f32), jax.Sh...]
where the time goes in v2:
time: 210 us
  Pallas kernels  204 us (97%)
  local copies, waits for them, and re-layouts  3.39 us (2%)
  between operations  2.39 us (1%)
    pallas_call x1, Pallas kernels, device_body(): pl.pallas_call(kernel, out_shape=(jax.ShapeDtypeStruct((1,), f32), jax.Sh...  204 us

profile of v2, /device:TPU:0, one launch (start us, length us, event | category | flops | bytes accessed | tf_op | source)
XLA Modules:
  0.0 209.6 jit_solution(7147798058602023716)
XLA Ops:
  0.6 203.9 %qaoa.1 = (f32[1]{0:T(128)}, f32[8,256,128]{2,1,0:T(8,128)}, f32[8,256,128]{2,1,0:T(8,128)}) custom-call(f32[8,256,128]{2,1,0:T(8,128)} %bitcast.3, f32[8]{0:T(128)} %gammas.1, f32[8]{0:T(128)} %betas.1), custom_call_target="tpu_custom_call" | custom-call | tf_op jit(solution)/shard_map/qaoa/pallas_call | solution.py:295
  205.1 0.0 copy-start
  205.1 2.4 %copy.10 = f32[262144]{0:T(1024)} copy(f32[262144]{0:T(1024)} %bitcast.5) | data formatting | bytes 2097152
  207.5 0.0 copy-done
  207.5 1.0 copy.11
Async XLA Ops:
  205.1 2.4 %copy-start = (f32[8,256,128]{2,1,0:T(8,128)S(1)}, f32[8,256,128]{2,1,0:T(8,128)}, u32[]{:S(2)}) copy-start(f32[8,256,128]{2,1,0:T(8,128)} %get-tuple-element.8) | copy-start | bytes 3145732

commit v3 on v2

--- a/solution.py
+++ b/solution.py
@@ -7,7 +7,7 @@
 
 LANES = 128
 LAYERS = 8
-SUB = 2
+SUB = 4
 PER_SUB = 8 // SUB
 
 
@@ -59,9 +59,11 @@
     return real, imag
 
 
-def kernel(cost, gammas, betas, energy, out_re, out_im,
-           cost_swap, recv, send, work, cos_buf, sin_buf, rows_in, matrix,
-           energy_part, energy_all, cost_send, cost_recv, send_sem, recv_sem, e_send, e_recv):
+def kernel(cost_hbm, gammas, betas, energy_all, out_re, out_im,
+           cost, cost_swap, recv, send, work, cos_buf, sin_buf, rows_in, matrix,
+           energy_part, cost_in, cost_send, cost_recv, send_sem, recv_sem, e_send, e_recv):
+    load = pltpu.make_async_copy(cost_hbm, cost, cost_in)
+    load.start()
     qx = lax.axis_index('qx')
     qy = lax.axis_index('qy')
     bits = (qy, qx % 2, qx // 2)
@@ -81,6 +83,7 @@
     for offset in range(1, 8):
         pl.semaphore_signal(barrier, inc=1, device_id=peer(offset), device_id_type=pl.DeviceIdType.MESH)
     pl.semaphore_wait(barrier, 7)
+    load.wait()
 
     for offset in range(1, 8):
         pltpu.make_async_remote_copy(
@@ -274,10 +277,18 @@
     for offset in range(1, 8):
         pltpu.make_async_copy(energy_part, energy_part, e_send.at[offset]).wait()
         pltpu.make_async_copy(energy_part, energy_part, e_recv.at[offset]).wait()
+
+
+def write_out(energy_all, in_re, in_im, energy, out_re, out_im, sem):
+    copies = [pltpu.make_async_copy(in_re, out_re, sem.at[0]), pltpu.make_async_copy(in_im, out_im, sem.at[1])]
+    for copy in copies:
+        copy.start()
     total = energy_all[0]
     for i in range(1, 8):
         total = total + energy_all[i]
     energy[0] = jnp.sum(total) * (1.0 / (1 << 21))
+    for copy in copies:
+        copy.wait()
 
 
 def solution(mesh):
@@ -292,26 +303,35 @@
         smem = pl.BlockSpec(memory_space=pltpu.SMEM)
         dma = pltpu.SemaphoreType.DMA
         parts = (2, 2, 2, SUB, 8, 2, 8 * PER_SUB, LANES)
-        energy, state_re, state_im = pl.pallas_call(
+        hbm = pl.BlockSpec(memory_space=pl.ANY)
+        results = pl.pallas_call(
             kernel,
-            out_shape=(jax.ShapeDtypeStruct((1,), f32),
-                       jax.ShapeDtypeStruct(shape, f32), jax.ShapeDtypeStruct(shape, f32)),
-            in_specs=[vmem, smem, smem],
-            out_specs=(smem, vmem, vmem),
+            out_shape=(pltpu.VMEM((8, 8, LANES), f32), pltpu.VMEM(shape, f32), pltpu.VMEM(shape, f32)),
+            in_specs=[hbm, smem, smem],
+            out_specs=(vmem, vmem, vmem),
             scratch_shapes=[
-                pltpu.VMEM(shape, f32),
+                pltpu.VMEM(shape, f32), pltpu.VMEM(shape, f32),
                 pltpu.VMEM(parts, f32), pltpu.VMEM(parts, f32),
                 pltpu.VMEM((4, 2 * LANES, 2 * LANES), f32),
                 pltpu.VMEM((16, 64, LANES), f32), pltpu.VMEM((16, 64, LANES), f32),
                 pltpu.VMEM((2 * LANES, 2 * LANES), f32), pltpu.VMEM((2 * LANES, 2 * LANES), f32),
-                pltpu.VMEM((8, LANES), f32), pltpu.VMEM((8, 8, LANES), f32),
-                dma, dma,
+                pltpu.VMEM((8, LANES), f32),
+                dma, dma, dma,
                 dma((2, 2, 2, SUB)), dma((2, 2, 2, SUB)),
                 dma((8,)), dma((8,)),
             ],
             compiler_params=pltpu.CompilerParams(collective_id=0, has_side_effects=True),
             name='qaoa',
         )(cost_local.reshape(shape), gammas, betas)
+        energy, state_re, state_im = pl.pallas_call(
+            write_out,
+            out_shape=(jax.ShapeDtypeStruct((1,), f32),
+                       jax.ShapeDtypeStruct(shape, f32), jax.ShapeDtypeStruct(shape, f32)),
+            in_specs=[vmem, vmem, vmem],
+            out_specs=(smem, hbm, hbm),
+            scratch_shapes=[dma((2,))],
+            name='write_out',
+        )(*[pltpu.with_memory_space_constraint(value, pltpu.VMEM) for value in results])
         return energy, state_re.reshape(local_len), state_im.reshape(local_len)
 
     return jax.shard_map(device_body, mesh=mesh, in_specs=(state_spec, P(), P()),

time: 210 us -> 205 us (0.976)
  local copies, waits for them, and re-layouts: 3.39 us -> 0 us
    unnamed x4 -> x0, local copies, waits for them, and re-layouts: 3.39 us -> none
    pallas_call x1 -> x2, Pallas kernels: 204 us -> 204 us  [the longest x1 202 us: device_body(): pl.pallas_call(kernel, out_shape=(pltpu.VMEM((8, 8, LANES), f32), pltpu.V...]
where the time goes in v3:
time: 205 us
  Pallas kernels  204 us (100%)
    pallas_call x1, Pallas kernels, device_body(): pl.pallas_call(kernel, out_shape=(pltpu.VMEM((8, 8, LANES), f32), pltpu.V...  202 us

profile of v3, /device:TPU:0, one launch (start us, length us, event | category | flops | bytes accessed | tf_op | source)
XLA Modules:
  0.0 204.6 jit_solution(118854959242051626)
XLA Ops:
  0.6 202.1 %qaoa.1 = (f32[8,8,128]{2,1,0:T(8,128)S(1)}, f32[8,256,128]{2,1,0:T(8,128)S(1)}, f32[8,256,128]{2,1,0:T(8,128)S(1)}) custom-call(f32[8,256,128]{2,1,0:T(8,128)} %bitcast.3, f32[8]{0:T(128)} %gammas.1, f32[8]{0:T(128)} %betas.1), custom_call_target="tpu_custom_call" | custom-call | tf_op jit(solution)/shard_map/qaoa/pallas_call | solution.py:307
  202.7 1.9 write_out.1

commit v4 on v3

--- a/solution.py
+++ b/solution.py
@@ -9,6 +9,7 @@
 LAYERS = 8
 SUB = 4
 PER_SUB = 8 // SUB
+SEND_ORDER = (5, 7, 4, 6, 1, 3, 2)
 
 
 def rotate(re, im, cos_half, sin_half):
@@ -199,7 +200,7 @@
 
                 lax.fori_loop(1, 8, body, 0)
                 for sub in range(SUB):
-                    for offset in range(1, 8):
+                    for offset in SEND_ORDER:
                         pltpu.make_async_remote_copy(
                             src_ref=send.at[target, a, b, sub, offset],
                             dst_ref=recv.at[target, a, b, sub, offset],
@@ -280,7 +281,8 @@
 
 
 def write_out(energy_all, in_re, in_im, energy, out_re, out_im, sem):
-    copies = [pltpu.make_async_copy(in_re, out_re, sem.at[0]), pltpu.make_async_copy(in_im, out_im, sem.at[1])]
+    copies = [pltpu.make_async_copy(source.at[i], result.at[i], sem.at[c, i])
+              for i in range(8) for c, (source, result) in enumerate(((in_re, out_re), (in_im, out_im)))]
     for copy in copies:
         copy.start()
     total = energy_all[0]
@@ -329,7 +331,7 @@
                        jax.ShapeDtypeStruct(shape, f32), jax.ShapeDtypeStruct(shape, f32)),
             in_specs=[vmem, vmem, vmem],
             out_specs=(smem, hbm, hbm),
-            scratch_shapes=[dma((2,))],
+            scratch_shapes=[dma((2, 8))],
             name='write_out',
         )(*[pltpu.with_memory_space_constraint(value, pltpu.VMEM) for value in results])
         return energy, state_re.reshape(local_len), state_im.reshape(local_len)

time: 205 us -> 205 us (level)
  no operation moved by 1% of the time
where the time goes in v4:
time: 205 us; the launch traced here: 204 us
  Pallas kernels  204 us (100%)
    pallas_call x1, Pallas kernels, device_body(): pl.pallas_call(kernel, out_shape=(pltpu.VMEM((8, 8, LANES), f32), pltpu.V...  202 us

profile of v4, /device:TPU:0, one launch (start us, length us, event | category | flops | bytes accessed | tf_op | source)
XLA Modules:
  0.0 204.4 jit_solution(3726266850961740643)
XLA Ops:
  0.6 201.8 %qaoa.1 = (f32[8,8,128]{2,1,0:T(8,128)S(1)}, f32[8,256,128]{2,1,0:T(8,128)S(1)}, f32[8,256,128]{2,1,0:T(8,128)S(1)}) custom-call(f32[8,256,128]{2,1,0:T(8,128)} %bitcast.3, f32[8]{0:T(128)} %gammas.1, f32[8]{0:T(128)} %betas.1), custom_call_target="tpu_custom_call" | custom-call | tf_op jit(solution)/shard_map/qaoa/pallas_call | solution.py:309
  202.4 2.0 write_out.1

commit v5 on v3

v5 whole, which is shorter than its diff:
```python
import jax
import jax.numpy as jnp
from jax import lax
from jax.experimental import pallas as pl
from jax.experimental.pallas import tpu as pltpu
from jax.sharding import PartitionSpec as P

LANES = 128
LAYERS = 8
SUB = 4
PER_SUB = 8 // SUB
SEND_ORDER = (5, 7, 4, 6, 1, 3, 2)
NEAR = (4, 1)


def rotate(re, im, cos_half, sin_half, steps=None):
    count = len(re)
    for step in steps or [1 << i for i in range(count.bit_length() - 1)]:
        new_re = [cos_half * re[i] + sin_half * im[i ^ step] for i in range(count)]
        new_im = [cos_half * im[i] - sin_half * re[i ^ step] for i in range(count)]
        re, im = new_re, new_im
    return re, im


def sublane_rotate(re, im, cos_half, sin_half):
    row = lax.broadcasted_iota(jnp.int32, (8, LANES), 0)
    for step in (1, 2, 4):
        bit_set = (row & step) != 0

        def flip(value):
            down = pltpu.roll(value, step, 0)
            if step == 4:
                return down
            return jnp.where(bit_set, down, pltpu.roll(value, 8 - step, 0))

        flip_re = [flip(value) for value in re]
        flip_im = [flip(value) for value in im]
        re, im = ([cos_half * r + sin_half * fi for r, fi in zip(re, flip_im)],
                  [cos_half * i - sin_half * fr for i, fr in zip(im, flip_re)])
    return re, im


def lane_matrix(cos_half, sin_half):
    row = lax.broadcasted_iota(jnp.int32, (LANES, LANES), 0)
    col = lax.broadcasted_iota(jnp.int32, (LANES, LANES), 1)
    diff = row ^ col
    cos_full = jnp.broadcast_to(cos_half[0:1], (LANES, LANES))
    sin_full = jnp.broadcast_to(sin_half[0:1], (LANES, LANES))
    mag = jnp.ones((LANES, LANES), jnp.float32)
    weight = jnp.zeros((LANES, LANES), jnp.int32)
    for bit in range(7):
        on = (diff >> bit) & 1
        mag = mag * jnp.where(on == 1, sin_full, cos_full)
        weight = weight + on
    quarter = weight & 3
    zero = jnp.zeros_like(mag)
    real = jnp.where(quarter == 0, mag, jnp.where(quarter == 2, -mag, zero))
    imag = jnp.where(quarter == 1, -mag, jnp.where(quarter == 3, mag, zero))
    return real, imag


def kernel(cost_hbm, gammas, betas, energy_all, out_re, out_im,
           cost, cost_near, cost_swap, recv, send, work, cos_buf, sin_buf, cos_near, sin_near,
           rows_in, matrix, energy_part, cost_in, near_send, near_recv, cost_send, cost_recv,
           send_sem, recv_sem, e_send, e_recv):
    load = pltpu.make_async_copy(cost_hbm, cost, cost_in)
    load.start()
    qx = lax.axis_index('qx')
    qy = lax.axis_index('qy')
    bits = (qy, qx % 2, qx // 2)

    def flipped(offset):
        return [1 - bit if (offset >> i) & 1 else bit for i, bit in enumerate(bits)]

    def block(offset):
        y, core, x = flipped(offset)
        return (x * 2 + core) * 2 + y

    def peer(offset):
        y, core, x = flipped(offset)
        return {'qy': y, 'qx': x * 2 + core}

    def remote(source, target, send_at, recv_at, offset):
        pltpu.make_async_remote_copy(
            src_ref=source, dst_ref=target, send_sem=send_at, recv_sem=recv_at,
            device_id=peer(offset), device_id_type=pl.DeviceIdType.MESH).start()

    barrier = pltpu.get_barrier_semaphore()
    for offset in range(1, 8):
        pl.semaphore_signal(barrier, inc=1, device_id=peer(offset), device_id_type=pl.DeviceIdType.MESH)
    pl.semaphore_wait(barrier, 7)
    load.wait()

    def half_angle(layer):
        angle = jnp.full((8, LANES), 0.5 * betas[layer], jnp.float32)
        return jnp.cos(angle), jnp.sin(angle)

    def wait_bytes(part, sem):
        pltpu.make_async_copy(part, part, sem).wait()

    def wait_all(buffer, sem, at, count):
        wait_bytes(buffer.at[(*at, pl.ds(0, count))], sem.at[at])

    def rows_of(r):
        return pl.ds(pl.multiple_of(r * 8, 8), 8)

    def set_matrix(cos_half, sin_half):
        real, imag = lane_matrix(cos_half, sin_half)
        matrix[0:LANES, 0:LANES] = real
        matrix[0:LANES, LANES:] = imag
        matrix[LANES:, 0:LANES] = -imag
        matrix[LANES:, LANES:] = real

    def put_rows(i, re, im):
        for o in range(16):
            at = pl.multiple_of(o * 16 + i * 8, 8)
            rows_in[pl.ds(at, 8), 0:LANES] = re[o]
            rows_in[pl.ds(at, 8), LANES:] = im[o]

    def lanes(a_held, at):
        work[a_held, at] = lax.dot(
            rows_in[...], matrix[...],
            precision=lax.Precision.HIGHEST, preferred_element_type=jnp.float32)

    def emit(held, mixed, target, a, b, cos_half, sin_half, order, route, local):
        def across(o, buffer):
            def part(r, c):
                at = pl.multiple_of((mixed * 8 + o) * 16 + (r % 2) * 8, 8)
                return work[held, r // 2, pl.ds(at, 8), c * LANES:(c + 1) * LANES]

            re = [part(r, 0) for r in range(8)]
            im = [part(r, 1) for r in range(8)]
            re, im = rotate(re, im, cos_half, sin_half)
            for r in range(8):
                row = (r % PER_SUB) * 8
                buffer[target, a, b, r // PER_SUB, o, 0, row:row + 8, :] = re[r]
                buffer[target, a, b, r // PER_SUB, o, 1, row:row + 8, :] = im[r]

        def body(o, carry):
            across(o, send)
            return carry

        lax.fori_loop(1, 8, body, 0)
        for sub in range(SUB):
            at = (target, a, b, sub)
            for o in order:
                remote(send.at[(*at, o)], recv.at[(*at, o)], send_sem.at[at], recv_sem.at[at], route(o))
        for o in local:
            across(o, recv)

    def first_layer():
        def sub_rows(sub):
            return pl.ds(pl.multiple_of(sub * 8 * PER_SUB, 8), 8 * PER_SUB)

        for sub in range(SUB):
            for a in range(2):
                remote(cost.at[:, a, :, sub_rows(sub)], cost_near.at[:, a, :, sub_rows(sub)],
                       near_send.at[a, sub], near_recv.at[a, sub], NEAR[a])
        for a in range(2):
            for o in range(1, 8):
                if not o & NEAR[a]:
                    remote(cost.at[block(o), a], cost_swap.at[o, a], cost_send, cost_recv, o)

        gamma = gammas[0]
        cos_half, sin_half = half_angle(0)
        set_matrix(cos_half, sin_half)

        def own_trig(r, carry):
            for a in range(2):
                for b in range(2):
                    for o in range(8):
                        angle = gamma * cost[block(o), a, b, rows_of(r), :]
                        cos_buf[a, b * 8 + o, rows_of(r), :] = jnp.cos(angle)
                        sin_buf[a, b * 8 + o, rows_of(r), :] = jnp.sin(angle)
            return carry

        lax.fori_loop(0, 8, own_trig, 0)

        def sub_step(sub, carry):
            for a in range(2):
                bit = NEAR[a]
                part = cost_near.at[:, a, :, sub_rows(sub)]
                wait_bytes(part, near_recv.at[a, sub])
                for o in range(1, 8):
                    if not o & bit:
                        remote(cost_near.at[block(o), a, :, sub_rows(sub)],
                               cost_swap.at[o | bit, a, :, sub_rows(sub)], cost_send, cost_recv, o)

                def slots(i, carry):
                    r = sub * PER_SUB + i
                    for b in range(2):
                        for o in range(8):
                            angle = gamma * cost_near[block(o), a, b, rows_of(r), :]
                            cos_near[b * 8 + o] = jnp.cos(angle)
                            sin_near[b * 8 + o] = jnp.sin(angle)
                    re, im = [None] * 16, [None] * 16
                    for b in range(2):
                        for o in range(8):
                            if o & bit:
                                continue
                            here, there = b * 8 + o, b * 8 + (o | bit)
                            for slot, cos_at, sin_at in (
                                    (here, lambda k: cos_buf[a, k, rows_of(r), :], lambda k: sin_buf[a, k, rows_of(r), :]),
                                    (there, lambda k: cos_near[k], lambda k: sin_near[k])):
                                re[slot] = cos_half * cos_at(here) - sin_half * sin_at(there)
                                im[slot] = -(cos_half * sin_at(here)) - sin_half * cos_at(there)
                    re, im = rotate(re, im, cos_half, sin_half, [step for step in (1, 2, 4, 8) if step != bit])
                    re, im = sublane_rotate(re, im, cos_half, sin_half)
                    put_rows(i, re, im)
                    return carry

                lax.fori_loop(0, PER_SUB, slots, 0)
                lanes(a, sub)
            return carry

        lax.fori_loop(0, SUB, sub_step, 0)

        def quarters(b, carry):
            for a in range(2):
                bit = NEAR[a]
                emit(a, b, 1, a, b, cos_half, sin_half,
                     [o for o in (3, 6, 7, 1, 4, 5, 2) if o & ~bit], lambda o: o & ~bit, (0, bit))
            return carry

        lax.fori_loop(0, 2, quarters, 0)
        cost_swap[0] = cost[block(0)]
        for a in range(2):
            cost_swap[NEAR[a], a] = cost_near[block(0), a]
        wait_bytes(cost_swap.at[pl.ds(0, 6)], cost_recv)

    def run_layer(layer, odd, arrived, drained):
        source, target = (0, 1) if odd else (1, 0)

        def quarter(held, mixed):
            return (held, mixed) if odd else (mixed, held)

        cos_half, sin_half = half_angle(layer)
        cos_prev, sin_prev = half_angle(layer - 1)
        gamma = gammas[layer]
        set_matrix(cos_half, sin_half)

        def half(held, carry):
            def trig(r, carry):
                for mixed in range(2):
                    for o in range(8):
                        at = (block(o) if odd else o, *quarter(held, mixed), rows_of(r))
                        angle = gamma * (cost if odd else cost_swap)[at]
                        cos_buf[held, mixed * 8 + o, rows_of(r), :] = jnp.cos(angle)
                        sin_buf[held, mixed * 8 + o, rows_of(r), :] = jnp.sin(angle)
                return carry

            lax.fori_loop(0, 8, trig, 0)

            def sub_step(sub, carry):
                for mixed in range(2):
                    wait_all(recv, recv_sem, (source, *quarter(held, mixed), sub), arrived)

                def slots(i, carry):
                    r = sub * PER_SUB + i
                    cos_phase = [cos_buf[held, o, rows_of(r), :] for o in range(16)]
                    sin_phase = [sin_buf[held, o, rows_of(r), :] for o in range(16)]
                    old = [[recv[(source, *quarter(held, mixed), sub, o, c, rows_of(i))]
                            for mixed in range(2) for o in range(8)] for c in range(2)]
                    old_re, old_im = rotate(*old, cos_prev, sin_prev)
                    re = [r * c + i * s for r, i, c, s in zip(old_re, old_im, cos_phase, sin_phase)]
                    im = [i * c - r * s for r, i, c, s in zip(old_re, old_im, cos_phase, sin_phase)]
                    re, im = rotate(re, im, cos_half, sin_half)
                    re, im = sublane_rotate(re, im, cos_half, sin_half)
                    put_rows(i, re, im)
                    return carry

                lax.fori_loop(0, PER_SUB, slots, 0)
                lanes(held, sub)
                return carry

            lax.fori_loop(0, SUB, sub_step, 0)

            if drained:
                for mixed in range(2):
                    for sub in range(SUB):
                        wait_all(send, send_sem, (target, *quarter(held, mixed), sub), drained)

            def quarters(mixed, carry):
                emit(held, mixed, target, *quarter(held, mixed), cos_half, sin_half, SEND_ORDER, lambda o: o, (0,))
                return carry

            lax.fori_loop(0, 2, quarters, 0)
            return carry

        lax.fori_loop(0, 2, half, 0)

    first_layer()
    run_layer(1, False, 6, 0)
    run_layer(2, True, 7, 6)

    def layer_pair(i, carry):
        run_layer(2 * i + 3, False, 7, 7)
        run_layer(2 * i + 4, True, 7, 7)
        return carry

    lax.fori_loop(0, LAYERS // 2 - 2, layer_pair, 0)
    run_layer(LAYERS - 1, False, 7, 7)

    cos_half, sin_half = half_angle(LAYERS - 1)
    energy_part[...] = jnp.zeros((8, LANES), jnp.float32)

    def final_half(a, carry):
        def final_sub(sub, carry):
            for b in range(2):
                wait_all(recv, recv_sem, (0, a, b, sub), 7)

            def slots(i, carry):
                r = sub * PER_SUB + i
                old = [[recv[0, a, b, sub, o, c, rows_of(i), :] for b in range(2) for o in range(8)]
                       for c in range(2)]
                re, im = rotate(*old, cos_half, sin_half)
                total = energy_part[...]
                for b in range(2):
                    for o in range(8):
                        at = (block(o), a, b, rows_of(r))
                        x, y = re[b * 8 + o], im[b * 8 + o]
                        out_re[at] = x
                        out_im[at] = y
                        total = total + cost[at] * (x * x + y * y)
                energy_part[...] = total
                return carry

            lax.fori_loop(0, PER_SUB, slots, 0)
            return carry

        lax.fori_loop(0, SUB, final_sub, 0)
        return carry

    lax.fori_loop(0, 2, final_half, 0)

    me = block(0)
    for offset in range(1, 8):
        remote(energy_part, energy_all.at[me], e_send.at[offset], e_recv.at[offset], offset)
    energy_all[me] = energy_part[...]
    for par in range(2):
        for a in range(2):
            for b in range(2):
                for sub in range(SUB):
                    wait_all(send, send_sem, (par, a, b, sub), 7)
    for a in range(2):
        for sub in range(SUB):
            wait_bytes(cost.at[:, a, :, pl.ds(sub * 8 * PER_SUB, 8 * PER_SUB)], near_send.at[a, sub])
    wait_bytes(cost_swap.at[pl.ds(0, 6)], cost_send)
    for offset in range(1, 8):
        wait_bytes(energy_part, e_send.at[offset])
        wait_bytes(energy_part, e_recv.at[offset])


def write_out(energy_all, in_re, in_im, energy, out_re, out_im, sem):
    copies = [pltpu.make_async_copy(in_re, out_re, sem.at[0]), pltpu.make_async_copy(in_im, out_im, sem.at[1])]
    for copy in copies:
        copy.start()
    total = energy_all[0]
    for i in range(1, 8):
        total = total + energy_all[i]
    energy[0] = jnp.sum(total) * (1.0 / (1 << 21))
    for copy in copies:
        copy.wait()


def solution(mesh):
    state_spec = P(('inst', 'qx', 'qy'))

    def device_body(cost_local, gammas, betas):
        local_len = cost_local.shape[0]
        shape = (8, 2, 2, local_len // (32 * LANES), LANES)
        f32 = jnp.float32
        vmem = pl.BlockSpec(memory_space=pltpu.VMEM)
        smem = pl.BlockSpec(memory_space=pltpu.SMEM)
        dma = pltpu.SemaphoreType.DMA
        parts = (2, 2, 2, SUB, 8, 2, 8 * PER_SUB, LANES)
        hbm = pl.BlockSpec(memory_space=pl.ANY)
        results = pl.pallas_call(
            kernel,
            out_shape=(pltpu.VMEM((8, 8, LANES), f32), pltpu.VMEM(shape, f32), pltpu.VMEM(shape, f32)),
            in_specs=[hbm, smem, smem],
            out_specs=(vmem, vmem, vmem),
            scratch_shapes=[
                pltpu.VMEM(shape, f32), pltpu.VMEM(shape, f32), pltpu.VMEM(shape, f32),
                pltpu.VMEM(parts, f32), pltpu.VMEM(parts, f32),
                pltpu.VMEM((2, 4, 2 * LANES, 2 * LANES), f32),
                pltpu.VMEM((2, 16, 64, LANES), f32), pltpu.VMEM((2, 16, 64, LANES), f32),
                pltpu.VMEM((16, 8, LANES), f32), pltpu.VMEM((16, 8, LANES), f32),
                pltpu.VMEM((2 * LANES, 2 * LANES), f32), pltpu.VMEM((2 * LANES, 2 * LANES), f32),
                pltpu.VMEM((8, LANES), f32),
                dma, dma((2, SUB)), dma((2, SUB)), dma, dma,
                dma((2, 2, 2, SUB)), dma((2, 2, 2, SUB)),
                dma((8,)), dma((8,)),
            ],
            compiler_params=pltpu.CompilerParams(collective_id=0, has_side_effects=True),
            name='qaoa',
        )(cost_local.reshape(shape), gammas, betas)
        energy, state_re, state_im = pl.pallas_call(
            write_out,
            out_shape=(jax.ShapeDtypeStruct((1,), f32),
                       jax.ShapeDtypeStruct(shape, f32), jax.ShapeDtypeStruct(shape, f32)),
            in_specs=[vmem, vmem, vmem],
            out_specs=(smem, hbm, hbm),
            scratch_shapes=[dma((2,))],
            name='write_out',
        )(*[pltpu.with_memory_space_constraint(value, pltpu.VMEM) for value in results])
        return energy, state_re.reshape(local_len), state_im.reshape(local_len)

    return jax.shard_map(device_body, mesh=mesh, in_specs=(state_spec, P(), P()),
                         out_specs=(P('inst'), state_spec, state_spec), check_vma=False)
```

time: 205 us -> 199 us (0.971)
  Pallas kernels: 204 us -> 198 us
    pallas_call x1, Pallas kernels: 202 us -> 196 us  [device_body(): pl.pallas_call(kernel, out_shape=(pltpu.VMEM((8, 8, LANES), f32), pltpu.V...]
where the time goes in v5:
time: 199 us
  Pallas kernels  198 us (99%)
    pallas_call x1, Pallas kernels, device_body(): pl.pallas_call(kernel, out_shape=(pltpu.VMEM((8, 8, LANES), f32), pltpu.V...  196 us

profile of v5, /device:TPU:0, one launch (start us, length us, event | category | flops | bytes accessed | tf_op | source)
XLA Modules:
  0.0 198.8 jit_solution(4553505415797002971)
XLA Ops:
  0.6 196.3 %qaoa.1 = (f32[8,8,128]{2,1,0:T(8,128)S(1)}, f32[8,2,2,64,128]{4,3,2,1,0:T(8,128)S(1)}, f32[8,2,2,64,128]{4,3,2,1,0:T(8,128)S(1)}) custom-call(f32[8,2,2,64,128]{4,3,2,1,0:T(8,128)} %bitcast.3, f32[8]{0:T(128)} %gammas.1, f32[8]{0:T(128)} %betas.1), custom_call_target="tpu_custom_call" | custom-call | tf_op jit(solution)/shard_map/qaoa/pallas_call | solution.py:378
  196.9 1.9 write_out.1

commit v6 on v5

--- a/solution.py
+++ b/solution.py
@@ -61,10 +61,13 @@
 
 def kernel(cost_hbm, gammas, betas, energy_all, out_re, out_im,
            cost, cost_near, cost_swap, recv, send, work, cos_buf, sin_buf, cos_near, sin_near,
-           rows_in, matrix, energy_part, cost_in, near_send, near_recv, cost_send, cost_recv,
+           rows_in, matrix, energy_part, energy_row, cost_in, near_send, near_recv, cost_send, cost_recv,
            send_sem, recv_sem, e_send, e_recv):
-    load = pltpu.make_async_copy(cost_hbm, cost, cost_in)
-    load.start()
+    loads = [pltpu.make_async_copy(cost_hbm.at[:, :, :, pl.ds(sub * 8 * PER_SUB, 8 * PER_SUB)],
+                                   cost.at[:, :, :, pl.ds(sub * 8 * PER_SUB, 8 * PER_SUB)], cost_in.at[sub])
+             for sub in range(SUB)]
+    for load in loads:
+        load.start()
     qx = lax.axis_index('qx')
     qy = lax.axis_index('qy')
     bits = (qy, qx % 2, qx // 2)
@@ -89,7 +92,6 @@
     for offset in range(1, 8):
         pl.semaphore_signal(barrier, inc=1, device_id=peer(offset), device_id_type=pl.DeviceIdType.MESH)
     pl.semaphore_wait(barrier, 7)
-    load.wait()
 
     def half_angle(layer):
         angle = jnp.full((8, LANES), 0.5 * betas[layer], jnp.float32)
@@ -153,6 +155,7 @@
             return pl.ds(pl.multiple_of(sub * 8 * PER_SUB, 8), 8 * PER_SUB)
 
         for sub in range(SUB):
+            loads[sub].wait()
             for a in range(2):
                 remote(cost.at[:, a, :, sub_rows(sub)], cost_near.at[:, a, :, sub_rows(sub)],
                        near_send.at[a, sub], near_recv.at[a, sub], NEAR[a])
@@ -334,9 +337,10 @@
     lax.fori_loop(0, 2, final_half, 0)
 
     me = block(0)
+    energy_row[...] = jnp.sum(energy_part[...], axis=0, keepdims=True)
     for offset in range(1, 8):
-        remote(energy_part, energy_all.at[me], e_send.at[offset], e_recv.at[offset], offset)
-    energy_all[me] = energy_part[...]
+        remote(energy_row, energy_all.at[me], e_send.at[offset], e_recv.at[offset], offset)
+    energy_all[me] = energy_row[...]
     for par in range(2):
         for a in range(2):
             for b in range(2):
@@ -347,18 +351,20 @@
             wait_bytes(cost.at[:, a, :, pl.ds(sub * 8 * PER_SUB, 8 * PER_SUB)], near_send.at[a, sub])
     wait_bytes(cost_swap.at[pl.ds(0, 6)], cost_send)
     for offset in range(1, 8):
-        wait_bytes(energy_part, e_send.at[offset])
-        wait_bytes(energy_part, e_recv.at[offset])
-
-
-def write_out(energy_all, in_re, in_im, energy, out_re, out_im, sem):
+        wait_bytes(energy_row, e_send.at[offset])
+        wait_bytes(energy_row, e_recv.at[offset])
+
+
+def write_out(energy_all, in_re, in_im, energy, out_re, out_im, value, sem):
     copies = [pltpu.make_async_copy(in_re, out_re, sem.at[0]), pltpu.make_async_copy(in_im, out_im, sem.at[1])]
     for copy in copies:
         copy.start()
     total = energy_all[0]
     for i in range(1, 8):
         total = total + energy_all[i]
-    energy[0] = jnp.sum(total) * (1.0 / (1 << 21))
+    value[0] = jnp.sum(total) * (1.0 / (1 << 21))
+    copies.append(pltpu.make_async_copy(value, energy, sem.at[2]))
+    copies[2].start()
     for copy in copies:
         copy.wait()
 
@@ -377,7 +383,7 @@
         hbm = pl.BlockSpec(memory_space=pl.ANY)
         results = pl.pallas_call(
             kernel,
-            out_shape=(pltpu.VMEM((8, 8, LANES), f32), pltpu.VMEM(shape, f32), pltpu.VMEM(shape, f32)),
+            out_shape=(pltpu.VMEM((8, 1, LANES), f32), pltpu.VMEM(shape, f32), pltpu.VMEM(shape, f32)),
             in_specs=[hbm, smem, smem],
             out_specs=(vmem, vmem, vmem),
             scratch_shapes=[
@@ -387,8 +393,8 @@
                 pltpu.VMEM((2, 16, 64, LANES), f32), pltpu.VMEM((2, 16, 64, LANES), f32),
                 pltpu.VMEM((16, 8, LANES), f32), pltpu.VMEM((16, 8, LANES), f32),
                 pltpu.VMEM((2 * LANES, 2 * LANES), f32), pltpu.VMEM((2 * LANES, 2 * LANES), f32),
-                pltpu.VMEM((8, LANES), f32),
-                dma, dma((2, SUB)), dma((2, SUB)), dma, dma,
+                pltpu.VMEM((8, LANES), f32), pltpu.VMEM((1, LANES), f32),
+                dma((SUB,)), dma((2, SUB)), dma((2, SUB)), dma, dma,
                 dma((2, 2, 2, SUB)), dma((2, 2, 2, SUB)),
                 dma((8,)), dma((8,)),
             ],
@@ -400,8 +406,8 @@
             out_shape=(jax.ShapeDtypeStruct((1,), f32),
                        jax.ShapeDtypeStruct(shape, f32), jax.ShapeDtypeStruct(shape, f32)),
             in_specs=[vmem, vmem, vmem],
-            out_specs=(smem, hbm, hbm),
-            scratch_shapes=[dma((2,))],
+            out_specs=(hbm, hbm, hbm),
+            scratch_shapes=[pltpu.SMEM((1,), f32), dma((3,))],
             name='write_out',
         )(*[pltpu.with_memory_space_constraint(value, pltpu.VMEM) for value in results])
         return energy, state_re.reshape(local_len), state_im.reshape(local_len)

time: 199 us -> 198 us (level)
  no operation moved by 1% of the time
where the time goes in v6:
time: 198 us
  Pallas kernels  198 us (100%)
    pallas_call x1, Pallas kernels, device_body(): pl.pallas_call(kernel, out_shape=(pltpu.VMEM((8, 1, LANES), f32), pltpu.V...  196 us

profile of v6, /device:TPU:0, one launch (start us, length us, event | category | flops | bytes accessed | tf_op | source)
XLA Modules:
  0.0 198.3 jit_solution(4020194032384090418)
XLA Ops:
  0.6 196.3 %qaoa.1 = (f32[8,1,128]{2,1,0:T(1,128)S(1)}, f32[8,2,2,64,128]{4,3,2,1,0:T(8,128)S(1)}, f32[8,2,2,64,128]{4,3,2,1,0:T(8,128)S(1)}) custom-call(f32[8,2,2,64,128]{4,3,2,1,0:T(8,128)} %bitcast.3, f32[8]{0:T(128)} %gammas.1, f32[8]{0:T(128)} %betas.1), custom_call_target="tpu_custom_call" | custom-call | tf_op jit(solution)/shard_map/qaoa/pallas_call | solution.py:384
  196.9 1.4 write_out.1

commit v7 on v6

--- a/solution.py
+++ b/solution.py
@@ -59,14 +59,18 @@
     return real, imag
 
 
-def kernel(cost_hbm, gammas, betas, energy_all, out_re, out_im,
+def kernel(cost_hbm, gammas_hbm, betas_hbm, energy_all, out_re, out_im,
            cost, cost_near, cost_swap, recv, send, work, cos_buf, sin_buf, cos_near, sin_near,
-           rows_in, matrix, energy_part, energy_row, cost_in, near_send, near_recv, cost_send, cost_recv,
+           rows_in, matrix, energy_part, energy_row, gammas, betas, angle_in, cost_in, near_send, near_recv, cost_send, cost_recv,
            send_sem, recv_sem, e_send, e_recv):
     loads = [pltpu.make_async_copy(cost_hbm.at[:, :, :, pl.ds(sub * 8 * PER_SUB, 8 * PER_SUB)],
                                    cost.at[:, :, :, pl.ds(sub * 8 * PER_SUB, 8 * PER_SUB)], cost_in.at[sub])
              for sub in range(SUB)]
     for load in loads:
+        load.start()
+    angle_loads = [pltpu.make_async_copy(gammas_hbm, gammas, angle_in.at[0]),
+                   pltpu.make_async_copy(betas_hbm, betas, angle_in.at[1])]
+    for load in angle_loads:
         load.start()
     qx = lax.axis_index('qx')
     qy = lax.axis_index('qy')
@@ -164,6 +168,8 @@
                 if not o & NEAR[a]:
                     remote(cost.at[block(o), a], cost_swap.at[o, a], cost_send, cost_recv, o)
 
+        for load in angle_loads:
+            load.wait()
         gamma = gammas[0]
         cos_half, sin_half = half_angle(0)
         set_matrix(cos_half, sin_half)
@@ -377,14 +383,13 @@
         shape = (8, 2, 2, local_len // (32 * LANES), LANES)
         f32 = jnp.float32
         vmem = pl.BlockSpec(memory_space=pltpu.VMEM)
-        smem = pl.BlockSpec(memory_space=pltpu.SMEM)
         dma = pltpu.SemaphoreType.DMA
         parts = (2, 2, 2, SUB, 8, 2, 8 * PER_SUB, LANES)
         hbm = pl.BlockSpec(memory_space=pl.ANY)
         results = pl.pallas_call(
             kernel,
             out_shape=(pltpu.VMEM((8, 1, LANES), f32), pltpu.VMEM(shape, f32), pltpu.VMEM(shape, f32)),
-            in_specs=[hbm, smem, smem],
+            in_specs=[hbm, hbm, hbm],
             out_specs=(vmem, vmem, vmem),
             scratch_shapes=[
                 pltpu.VMEM(shape, f32), pltpu.VMEM(shape, f32), pltpu.VMEM(shape, f32),
@@ -394,6 +399,7 @@
                 pltpu.VMEM((16, 8, LANES), f32), pltpu.VMEM((16, 8, LANES), f32),
                 pltpu.VMEM((2 * LANES, 2 * LANES), f32), pltpu.VMEM((2 * LANES, 2 * LANES), f32),
                 pltpu.VMEM((8, LANES), f32), pltpu.VMEM((1, LANES), f32),
+                pltpu.SMEM((LAYERS,), f32), pltpu.SMEM((LAYERS,), f32), dma((2,)),
                 dma((SUB,)), dma((2, SUB)), dma((2, SUB)), dma, dma,
                 dma((2, 2, 2, SUB)), dma((2, 2, 2, SUB)),
                 dma((8,)), dma((8,)),

time: 198 us -> 198 us (level)
  no operation moved by 1% of the time
where the time goes in v7:
time: 198 us
  Pallas kernels  197 us (99%)
    pallas_call x1, Pallas kernels, device_body(): pl.pallas_call(kernel, out_shape=(pltpu.VMEM((8, 1, LANES), f32), pltpu.V...  196 us

profile of v7, /device:TPU:0, one launch (start us, length us, event | category | flops | bytes accessed | tf_op | source)
XLA Modules:
  0.0 197.6 jit_solution(5426791351035918714)
XLA Ops:
  0.6 195.6 %qaoa.1 = (f32[8,1,128]{2,1,0:T(1,128)S(1)}, f32[8,2,2,64,128]{4,3,2,1,0:T(8,128)S(1)}, f32[8,2,2,64,128]{4,3,2,1,0:T(8,128)S(1)}) custom-call(f32[8,2,2,64,128]{4,3,2,1,0:T(8,128)} %bitcast.3, f32[8]{0:T(128)} %gammas_hbm.1, f32[8]{0:T(128)} %betas_hbm.1), custom_call_target="tpu_custom_call" | custom-call | tf_op jit(solution)/shard_map/qaoa/pallas_call | solution.py:389
  196.3 1.4 write_out.1

commit v8 on v7

--- a/solution.py
+++ b/solution.py
@@ -9,7 +9,7 @@
 LAYERS = 8
 SUB = 4
 PER_SUB = 8 // SUB
-SEND_ORDER = (5, 7, 4, 6, 1, 3, 2)
+SEND_ORDER = (1, 3, 2)
 NEAR = (4, 1)
 
 
@@ -151,6 +151,16 @@
             at = (target, a, b, sub)
             for o in order:
                 remote(send.at[(*at, o)], recv.at[(*at, o)], send_sem.at[at], recv_sem.at[at], route(o))
+            if len(local) == 1:
+                y, core, x = bits
+                for turn in (1 - core, core):
+                    for across_core in range(2):
+                        o = 4 + 2 * across_core + turn
+                        pltpu.make_async_remote_copy(
+                            src_ref=send.at[(*at, o)], dst_ref=recv.at[(*at, o)],
+                            send_sem=send_sem.at[at], recv_sem=recv_sem.at[at],
+                            device_id={'qy': (y + turn) % 2, 'qx': (1 - x) * 2 + (core + across_core) % 2},
+                            device_id_type=pl.DeviceIdType.MESH).start()
         for o in local:
             across(o, recv)
 

time: 198 us -> 198 us (level)
  no operation moved by 1% of the time
where the time goes in v8:
time: 198 us
  Pallas kernels  197 us (99%)
    pallas_call x1, Pallas kernels, device_body(): pl.pallas_call(kernel, out_shape=(pltpu.VMEM((8, 1, LANES), f32), pltpu.V...  196 us

profile of v8, /device:TPU:0, one launch (start us, length us, event | category | flops | bytes accessed | tf_op | source)
XLA Modules:
  0.0 197.8 jit_solution(16420323944361284244)
XLA Ops:
  0.6 195.8 %qaoa.1 = (f32[8,1,128]{2,1,0:T(1,128)S(1)}, f32[8,2,2,64,128]{4,3,2,1,0:T(8,128)S(1)}, f32[8,2,2,64,128]{4,3,2,1,0:T(8,128)S(1)}) custom-call(f32[8,2,2,64,128]{4,3,2,1,0:T(8,128)} %bitcast.3, f32[8]{0:T(128)} %gammas_hbm.1, f32[8]{0:T(128)} %betas_hbm.1), custom_call_target="tpu_custom_call" | custom-call | tf_op jit(solution)/shard_map/qaoa/pallas_call | solution.py:399
  196.4 1.4 write_out.1

commit v9 on v7

--- a/solution.py
+++ b/solution.py
@@ -61,7 +61,7 @@
 
 def kernel(cost_hbm, gammas_hbm, betas_hbm, energy_all, out_re, out_im,
            cost, cost_near, cost_swap, recv, send, work, cos_buf, sin_buf, cos_near, sin_near,
-           rows_in, matrix, energy_part, energy_row, gammas, betas, angle_in, cost_in, near_send, near_recv, cost_send, cost_recv,
+           rows_in, matrix, energy_part, energy_row, gammas, betas, angle_in, near_in, cost_in, near_send, near_recv, cost_send, cost_recv,
            send_sem, recv_sem, e_send, e_recv):
     loads = [pltpu.make_async_copy(cost_hbm.at[:, :, :, pl.ds(sub * 8 * PER_SUB, 8 * PER_SUB)],
                                    cost.at[:, :, :, pl.ds(sub * 8 * PER_SUB, 8 * PER_SUB)], cost_in.at[sub])
@@ -93,9 +93,12 @@
             device_id=peer(offset), device_id_type=pl.DeviceIdType.MESH).start()
 
     barrier = pltpu.get_barrier_semaphore()
-    for offset in range(1, 8):
-        pl.semaphore_signal(barrier, inc=1, device_id=peer(offset), device_id_type=pl.DeviceIdType.MESH)
-    pl.semaphore_wait(barrier, 7)
+    def signal_next(sem):
+        for offset in (4, 1, 2):
+            pl.semaphore_signal(sem, inc=1, device_id=peer(offset), device_id_type=pl.DeviceIdType.MESH)
+
+    signal_next(barrier)
+    pl.semaphore_wait(barrier, 3)
 
     def half_angle(layer):
         angle = jnp.full((8, LANES), 0.5 * betas[layer], jnp.float32)
@@ -147,12 +150,12 @@
             return carry
 
         lax.fori_loop(1, 8, body, 0)
+        for o in local:
+            across(o, recv)
         for sub in range(SUB):
             at = (target, a, b, sub)
             for o in order:
                 remote(send.at[(*at, o)], recv.at[(*at, o)], send_sem.at[at], recv_sem.at[at], route(o))
-        for o in local:
-            across(o, recv)
 
     def first_layer():
         def sub_rows(sub):
@@ -163,11 +166,7 @@
             for a in range(2):
                 remote(cost.at[:, a, :, sub_rows(sub)], cost_near.at[:, a, :, sub_rows(sub)],
                        near_send.at[a, sub], near_recv.at[a, sub], NEAR[a])
-        for a in range(2):
-            for o in range(1, 8):
-                if not o & NEAR[a]:
-                    remote(cost.at[block(o), a], cost_swap.at[o, a], cost_send, cost_recv, o)
-
+        signal_next(near_in.at[0])
         for load in angle_loads:
             load.wait()
         gamma = gammas[0]
@@ -183,7 +182,15 @@
                         sin_buf[a, b * 8 + o, rows_of(r), :] = jnp.sin(angle)
             return carry
 
-        lax.fori_loop(0, 8, own_trig, 0)
+        for round_id in range(2):
+            lax.fori_loop(4 * round_id, 4 * round_id + 4, own_trig, 0)
+            pl.semaphore_wait(near_in.at[round_id], 3)
+            if round_id == 0:
+                signal_next(near_in.at[1])
+        for a in range(2):
+            for o in range(1, 8):
+                if not o & NEAR[a]:
+                    remote(cost.at[block(o), a], cost_swap.at[o, a], cost_send, cost_recv, o)
 
         def sub_step(sub, carry):
             for a in range(2):
@@ -399,7 +406,7 @@
                 pltpu.VMEM((16, 8, LANES), f32), pltpu.VMEM((16, 8, LANES), f32),
                 pltpu.VMEM((2 * LANES, 2 * LANES), f32), pltpu.VMEM((2 * LANES, 2 * LANES), f32),
                 pltpu.VMEM((8, LANES), f32), pltpu.VMEM((1, LANES), f32),
-                pltpu.SMEM((LAYERS,), f32), pltpu.SMEM((LAYERS,), f32), dma((2,)),
+                pltpu.SMEM((LAYERS,), f32), pltpu.SMEM((LAYERS,), f32), dma((2,)), pltpu.SemaphoreType.REGULAR((2,)),
                 dma((SUB,)), dma((2, SUB)), dma((2, SUB)), dma, dma,
                 dma((2, 2, 2, SUB)), dma((2, 2, 2, SUB)),
                 dma((8,)), dma((8,)),

time: 198 us -> 197 us (level)
  no operation moved by 1% of the time
where the time goes in v9:
time: 197 us
  Pallas kernels  196 us (99%)
    pallas_call x1, Pallas kernels, device_body(): pl.pallas_call(kernel, out_shape=(pltpu.VMEM((8, 1, LANES), f32), pltpu.V...  195 us

profile of v9, /device:TPU:0, one launch (start us, length us, event | category | flops | bytes accessed | tf_op | source)
XLA Modules:
  0.0 196.6 jit_solution(9433375655108421269)
XLA Ops:
  0.6 194.7 %qaoa.1 = (f32[8,1,128]{2,1,0:T(1,128)S(1)}, f32[8,2,2,64,128]{4,3,2,1,0:T(8,128)S(1)}, f32[8,2,2,64,128]{4,3,2,1,0:T(8,128)S(1)}) custom-call(f32[8,2,2,64,128]{4,3,2,1,0:T(8,128)} %bitcast.3, f32[8]{0:T(128)} %gammas_hbm.1, f32[8]{0:T(128)} %betas_hbm.1), custom_call_target="tpu_custom_call" | custom-call | tf_op jit(solution)/shard_map/qaoa/pallas_call | solution.py:396
  195.3 1.4 write_out.1

commit v10 on v9

--- a/solution.py
+++ b/solution.py
@@ -7,7 +7,7 @@
 
 LANES = 128
 LAYERS = 8
-SUB = 4
+SUB = 2
 PER_SUB = 8 // SUB
 SEND_ORDER = (5, 7, 4, 6, 1, 3, 2)
 NEAR = (4, 1)
@@ -222,11 +222,15 @@
                                 im[slot] = -(cos_half * sin_at(here)) - sin_half * cos_at(there)
                     re, im = rotate(re, im, cos_half, sin_half, [step for step in (1, 2, 4, 8) if step != bit])
                     re, im = sublane_rotate(re, im, cos_half, sin_half)
-                    put_rows(i, re, im)
+                    put_rows(i % 2, re, im)
                     return carry
 
-                lax.fori_loop(0, PER_SUB, slots, 0)
-                lanes(a, sub)
+                def blocks(k, carry):
+                    lax.fori_loop(2 * k, 2 * k + 2, slots, 0)
+                    lanes(a, sub * (PER_SUB // 2) + k)
+                    return carry
+
+                lax.fori_loop(0, PER_SUB // 2, blocks, 0)
             return carry
 
         lax.fori_loop(0, SUB, sub_step, 0)
@@ -282,11 +286,15 @@
                     im = [i * c - r * s for r, i, c, s in zip(old_re, old_im, cos_phase, sin_phase)]
                     re, im = rotate(re, im, cos_half, sin_half)
                     re, im = sublane_rotate(re, im, cos_half, sin_half)
-                    put_rows(i, re, im)
+                    put_rows(i % 2, re, im)
                     return carry
 
-                lax.fori_loop(0, PER_SUB, slots, 0)
-                lanes(held, sub)
+                def blocks(k, carry):
+                    lax.fori_loop(2 * k, 2 * k + 2, slots, 0)
+                    lanes(held, sub * (PER_SUB // 2) + k)
+                    return carry
+
+                lax.fori_loop(0, PER_SUB // 2, blocks, 0)
                 return carry
 
             lax.fori_loop(0, SUB, sub_step, 0)

time: 197 us -> 197 us (level)
  no operation moved by 1% of the time
where the time goes in v10:
time: 197 us
  Pallas kernels  197 us (100%)
    pallas_call x1, Pallas kernels, device_body(): pl.pallas_call(kernel, out_shape=(pltpu.VMEM((8, 1, LANES), f32), pltpu.V...  195 us

profile of v10, /device:TPU:0, one launch (start us, length us, event | category | flops | bytes accessed | tf_op | source)
XLA Modules:
  0.0 197.3 jit_solution(5602876701787923793)
XLA Ops:
  0.6 195.3 %qaoa.1 = (f32[8,1,128]{2,1,0:T(1,128)S(1)}, f32[8,2,2,64,128]{4,3,2,1,0:T(8,128)S(1)}, f32[8,2,2,64,128]{4,3,2,1,0:T(8,128)S(1)}) custom-call(f32[8,2,2,64,128]{4,3,2,1,0:T(8,128)} %bitcast.3, f32[8]{0:T(128)} %gammas_hbm.1, f32[8]{0:T(128)} %betas_hbm.1), custom_call_target="tpu_custom_call" | custom-call | tf_op jit(solution)/shard_map/qaoa/pallas_call | solution.py:404
  195.9 1.4 write_out.1

commit v11 on v9

--- a/solution.py
+++ b/solution.py
@@ -7,8 +7,7 @@
 
 LANES = 128
 LAYERS = 8
-SUB = 4
-PER_SUB = 8 // SUB
+PAIRS = 4
 SEND_ORDER = (5, 7, 4, 6, 1, 3, 2)
 NEAR = (4, 1)
 
@@ -63,9 +62,9 @@
            cost, cost_near, cost_swap, recv, send, work, cos_buf, sin_buf, cos_near, sin_near,
            rows_in, matrix, energy_part, energy_row, gammas, betas, angle_in, near_in, cost_in, near_send, near_recv, cost_send, cost_recv,
            send_sem, recv_sem, e_send, e_recv):
-    loads = [pltpu.make_async_copy(cost_hbm.at[:, :, :, pl.ds(sub * 8 * PER_SUB, 8 * PER_SUB)],
-                                   cost.at[:, :, :, pl.ds(sub * 8 * PER_SUB, 8 * PER_SUB)], cost_in.at[sub])
-             for sub in range(SUB)]
+    loads = [pltpu.make_async_copy(cost_hbm.at[:, :, :, pl.ds(sub * 16, 16)],
+                                   cost.at[:, :, :, pl.ds(sub * 16, 16)], cost_in.at[sub])
+             for sub in range(PAIRS)]
     for load in loads:
         load.start()
     angle_loads = [pltpu.make_async_copy(gammas_hbm, gammas, angle_in.at[0]),
@@ -141,9 +140,8 @@
             im = [part(r, 1) for r in range(8)]
             re, im = rotate(re, im, cos_half, sin_half)
             for r in range(8):
-                row = (r % PER_SUB) * 8
-                buffer[target, a, b, r // PER_SUB, o, 0, row:row + 8, :] = re[r]
-                buffer[target, a, b, r // PER_SUB, o, 1, row:row + 8, :] = im[r]
+                buffer[target, a, b, r, o, 0] = re[r]
+                buffer[target, a, b, r, o, 1] = im[r]
 
         def body(o, carry):
             across(o, send)
@@ -152,16 +150,16 @@
         lax.fori_loop(1, 8, body, 0)
         for o in local:
             across(o, recv)
-        for sub in range(SUB):
-            at = (target, a, b, sub)
+        for r in range(8):
+            at = (target, a, b, r)
             for o in order:
                 remote(send.at[(*at, o)], recv.at[(*at, o)], send_sem.at[at], recv_sem.at[at], route(o))
 
     def first_layer():
         def sub_rows(sub):
-            return pl.ds(pl.multiple_of(sub * 8 * PER_SUB, 8), 8 * PER_SUB)
-
-        for sub in range(SUB):
+            return pl.ds(pl.multiple_of(sub * 16, 8), 16)
+
+        for sub in range(PAIRS):
             loads[sub].wait()
             for a in range(2):
                 remote(cost.at[:, a, :, sub_rows(sub)], cost_near.at[:, a, :, sub_rows(sub)],
@@ -203,7 +201,7 @@
                                cost_swap.at[o | bit, a, :, sub_rows(sub)], cost_send, cost_recv, o)
 
                 def slots(i, carry):
-                    r = sub * PER_SUB + i
+                    r = 2 * sub + i
                     for b in range(2):
                         for o in range(8):
                             angle = gamma * cost_near[block(o), a, b, rows_of(r), :]
@@ -225,11 +223,11 @@
                     put_rows(i, re, im)
                     return carry
 
-                lax.fori_loop(0, PER_SUB, slots, 0)
+                lax.fori_loop(0, 2, slots, 0)
                 lanes(a, sub)
             return carry
 
-        lax.fori_loop(0, SUB, sub_step, 0)
+        lax.fori_loop(0, PAIRS, sub_step, 0)
 
         def quarters(b, carry):
             for a in range(2):
@@ -268,14 +266,15 @@
             lax.fori_loop(0, 8, trig, 0)
 
             def sub_step(sub, carry):
-                for mixed in range(2):
-                    wait_all(recv, recv_sem, (source, *quarter(held, mixed), sub), arrived)
+                for i in range(2):
+                    for mixed in range(2):
+                        wait_all(recv, recv_sem, (source, *quarter(held, mixed), 2 * sub + i), arrived)
 
                 def slots(i, carry):
-                    r = sub * PER_SUB + i
+                    r = 2 * sub + i
                     cos_phase = [cos_buf[held, o, rows_of(r), :] for o in range(16)]
                     sin_phase = [sin_buf[held, o, rows_of(r), :] for o in range(16)]
-                    old = [[recv[(source, *quarter(held, mixed), sub, o, c, rows_of(i))]
+                    old = [[recv[(source, *quarter(held, mixed), r, o, c)]
                             for mixed in range(2) for o in range(8)] for c in range(2)]
                     old_re, old_im = rotate(*old, cos_prev, sin_prev)
                     re = [r * c + i * s for r, i, c, s in zip(old_re, old_im, cos_phase, sin_phase)]
@@ -285,16 +284,16 @@
                     put_rows(i, re, im)
                     return carry
 
-                lax.fori_loop(0, PER_SUB, slots, 0)
+                lax.fori_loop(0, 2, slots, 0)
                 lanes(held, sub)
                 return carry
 
-            lax.fori_loop(0, SUB, sub_step, 0)
+            lax.fori_loop(0, PAIRS, sub_step, 0)
 
             if drained:
                 for mixed in range(2):
-                    for sub in range(SUB):
-                        wait_all(send, send_sem, (target, *quarter(held, mixed), sub), drained)
+                    for r in range(8):
+                        wait_all(send, send_sem, (target, *quarter(held, mixed), r), drained)
 
             def quarters(mixed, carry):
                 emit(held, mixed, target, *quarter(held, mixed), cos_half, sin_half, SEND_ORDER, lambda o: o, (0,))
@@ -321,30 +320,23 @@
     energy_part[...] = jnp.zeros((8, LANES), jnp.float32)
 
     def final_half(a, carry):
-        def final_sub(sub, carry):
+        def slots(r, carry):
             for b in range(2):
-                wait_all(recv, recv_sem, (0, a, b, sub), 7)
-
-            def slots(i, carry):
-                r = sub * PER_SUB + i
-                old = [[recv[0, a, b, sub, o, c, rows_of(i), :] for b in range(2) for o in range(8)]
-                       for c in range(2)]
-                re, im = rotate(*old, cos_half, sin_half)
-                total = energy_part[...]
-                for b in range(2):
-                    for o in range(8):
-                        at = (block(o), a, b, rows_of(r))
-                        x, y = re[b * 8 + o], im[b * 8 + o]
-                        out_re[at] = x
-                        out_im[at] = y
-                        total = total + cost[at] * (x * x + y * y)
-                energy_part[...] = total
-                return carry
-
-            lax.fori_loop(0, PER_SUB, slots, 0)
-            return carry
-
-        lax.fori_loop(0, SUB, final_sub, 0)
+                wait_all(recv, recv_sem, (0, a, b, r), 7)
+            old = [[recv[0, a, b, r, o, c] for b in range(2) for o in range(8)] for c in range(2)]
+            re, im = rotate(*old, cos_half, sin_half)
+            total = energy_part[...]
+            for b in range(2):
+                for o in range(8):
+                    at = (block(o), a, b, rows_of(r))
+                    x, y = re[b * 8 + o], im[b * 8 + o]
+                    out_re[at] = x
+                    out_im[at] = y
+                    total = total + cost[at] * (x * x + y * y)
+            energy_part[...] = total
+            return carry
+
+        lax.fori_loop(0, 8, slots, 0)
         return carry
 
     lax.fori_loop(0, 2, final_half, 0)
@@ -357,11 +349,11 @@
     for par in range(2):
         for a in range(2):
             for b in range(2):
-                for sub in range(SUB):
-                    wait_all(send, send_sem, (par, a, b, sub), 7)
+                for r in range(8):
+                    wait_all(send, send_sem, (par, a, b, r), 7)
     for a in range(2):
-        for sub in range(SUB):
-            wait_bytes(cost.at[:, a, :, pl.ds(sub * 8 * PER_SUB, 8 * PER_SUB)], near_send.at[a, sub])
+        for sub in range(PAIRS):
+            wait_bytes(cost.at[:, a, :, pl.ds(sub * 16, 16)], near_send.at[a, sub])
     wait_bytes(cost_swap.at[pl.ds(0, 6)], cost_send)
     for offset in range(1, 8):
         wait_bytes(energy_row, e_send.at[offset])
@@ -391,7 +383,7 @@
         f32 = jnp.float32
         vmem = pl.BlockSpec(memory_space=pltpu.VMEM)
         dma = pltpu.SemaphoreType.DMA
-        parts = (2, 2, 2, SUB, 8, 2, 8 * PER_SUB, LANES)
+        parts = (2, 2, 2, 8, 8, 2, 8, LANES)
         hbm = pl.BlockSpec(memory_space=pl.ANY)
         results = pl.pallas_call(
             kernel,
@@ -407,8 +399,8 @@
                 pltpu.VMEM((2 * LANES, 2 * LANES), f32), pltpu.VMEM((2 * LANES, 2 * LANES), f32),
                 pltpu.VMEM((8, LANES), f32), pltpu.VMEM((1, LANES), f32),
                 pltpu.SMEM((LAYERS,), f32), pltpu.SMEM((LAYERS,), f32), dma((2,)), pltpu.SemaphoreType.REGULAR((2,)),
-                dma((SUB,)), dma((2, SUB)), dma((2, SUB)), dma, dma,
-                dma((2, 2, 2, SUB)), dma((2, 2, 2, SUB)),
+                dma((PAIRS,)), dma((2, PAIRS)), dma((2, PAIRS)), dma, dma,
+                dma((2, 2, 2, 8)), dma((2, 2, 2, 8)),
                 dma((8,)), dma((8,)),
             ],
             compiler_params=pltpu.CompilerParams(collective_id=0, has_side_effects=True),

time: 197 us -> 197 us (level)
  no operation moved by 1% of the time
where the time goes in v11:
time: 197 us
  Pallas kernels  197 us (100%)
    pallas_call x1, Pallas kernels, device_body(): pl.pallas_call(kernel, out_shape=(pltpu.VMEM((8, 1, LANES), f32), pltpu.V...  195 us

profile of v11, /device:TPU:0, one launch (start us, length us, event | category | flops | bytes accessed | tf_op | source)
XLA Modules:
  0.0 197.2 jit_solution(141794988654153686)
XLA Ops:
  0.6 195.2 %qaoa.1 = (f32[8,1,128]{2,1,0:T(1,128)S(1)}, f32[8,2,2,64,128]{4,3,2,1,0:T(8,128)S(1)}, f32[8,2,2,64,128]{4,3,2,1,0:T(8,128)S(1)}) custom-call(f32[8,2,2,64,128]{4,3,2,1,0:T(8,128)} %bitcast.3, f32[8]{0:T(128)} %gammas_hbm.1, f32[8]{0:T(128)} %betas_hbm.1), custom_call_target="tpu_custom_call" | custom-call | tf_op jit(solution)/shard_map/qaoa/pallas_call | solution.py:388
  195.9 1.4 write_out.1

commit v12 on v11

--- a/solution.py
+++ b/solution.py
@@ -7,6 +7,8 @@
 
 LANES = 128
 LAYERS = 8
+COARSE = 4
+FINE = 2
 PAIRS = 4
 SEND_ORDER = (5, 7, 4, 6, 1, 3, 2)
 NEAR = (4, 1)
@@ -106,8 +108,8 @@
     def wait_bytes(part, sem):
         pltpu.make_async_copy(part, part, sem).wait()
 
-    def wait_all(buffer, sem, at, count):
-        wait_bytes(buffer.at[(*at, pl.ds(0, count))], sem.at[at])
+    def wait_all(buffer, sem, at, first_r, size, count):
+        wait_bytes(buffer.at[(*at, pl.ds(0, count), pl.ds(0, size))], sem.at[(*at, first_r)])
 
     def rows_of(r):
         return pl.ds(pl.multiple_of(r * 8, 8), 8)
@@ -130,7 +132,7 @@
             rows_in[...], matrix[...],
             precision=lax.Precision.HIGHEST, preferred_element_type=jnp.float32)
 
-    def emit(held, mixed, target, a, b, cos_half, sin_half, order, route, local):
+    def emit(held, mixed, target, a, b, cos_half, sin_half, size, order, route, local):
         def across(o, buffer):
             def part(r, c):
                 at = pl.multiple_of((mixed * 8 + o) * 16 + (r % 2) * 8, 8)
@@ -140,8 +142,8 @@
             im = [part(r, 1) for r in range(8)]
             re, im = rotate(re, im, cos_half, sin_half)
             for r in range(8):
-                buffer[target, a, b, r, o, 0] = re[r]
-                buffer[target, a, b, r, o, 1] = im[r]
+                buffer[target, a, b, o, r, 0] = re[r]
+                buffer[target, a, b, o, r, 1] = im[r]
 
         def body(o, carry):
             across(o, send)
@@ -150,10 +152,11 @@
         lax.fori_loop(1, 8, body, 0)
         for o in local:
             across(o, recv)
-        for r in range(8):
-            at = (target, a, b, r)
+        for r in range(0, 8, size):
+            sem_at = (target, a, b, r)
             for o in order:
-                remote(send.at[(*at, o)], recv.at[(*at, o)], send_sem.at[at], recv_sem.at[at], route(o))
+                at = (target, a, b, o, pl.ds(r, size))
+                remote(send.at[at], recv.at[at], send_sem.at[sem_at], recv_sem.at[sem_at], route(o))
 
     def first_layer():
         def sub_rows(sub):
@@ -232,7 +235,7 @@
         def quarters(b, carry):
             for a in range(2):
                 bit = NEAR[a]
-                emit(a, b, 1, a, b, cos_half, sin_half,
+                emit(a, b, 1, a, b, cos_half, sin_half, COARSE,
                      [o for o in (3, 6, 7, 1, 4, 5, 2) if o & ~bit], lambda o: o & ~bit, (0, bit))
             return carry
 
@@ -242,7 +245,7 @@
             cost_swap[NEAR[a], a] = cost_near[block(0), a]
         wait_bytes(cost_swap.at[pl.ds(0, 6)], cost_recv)
 
-    def run_layer(layer, odd, arrived, drained):
+    def run_layer(layer, odd, arrived, drained, size=COARSE):
         source, target = (0, 1) if odd else (1, 0)
 
         def quarter(held, mixed):
@@ -265,16 +268,12 @@
 
             lax.fori_loop(0, 8, trig, 0)
 
-            def sub_step(sub, carry):
-                for i in range(2):
-                    for mixed in range(2):
-                        wait_all(recv, recv_sem, (source, *quarter(held, mixed), 2 * sub + i), arrived)
-
+            def block_step(sub):
                 def slots(i, carry):
                     r = 2 * sub + i
                     cos_phase = [cos_buf[held, o, rows_of(r), :] for o in range(16)]
                     sin_phase = [sin_buf[held, o, rows_of(r), :] for o in range(16)]
-                    old = [[recv[(source, *quarter(held, mixed), r, o, c)]
+                    old = [[recv[(source, *quarter(held, mixed), o, r, c)]
                             for mixed in range(2) for o in range(8)] for c in range(2)]
                     old_re, old_im = rotate(*old, cos_prev, sin_prev)
                     re = [r * c + i * s for r, i, c, s in zip(old_re, old_im, cos_phase, sin_phase)]
@@ -286,17 +285,27 @@
 
                 lax.fori_loop(0, 2, slots, 0)
                 lanes(held, sub)
+
+            def message(i, carry):
+                for mixed in range(2):
+                    wait_all(recv, recv_sem, (source, *quarter(held, mixed)), i * COARSE, COARSE, arrived)
+
+                def blocks(k, carry):
+                    block_step(i * (COARSE // 2) + k)
+                    return carry
+
+                lax.fori_loop(0, COARSE // 2, blocks, 0)
                 return carry
 
-            lax.fori_loop(0, PAIRS, sub_step, 0)
+            lax.fori_loop(0, 8 // COARSE, message, 0)
 
             if drained:
                 for mixed in range(2):
-                    for r in range(8):
-                        wait_all(send, send_sem, (target, *quarter(held, mixed), r), drained)
+                    for r in range(0, 8, COARSE):
+                        wait_all(send, send_sem, (target, *quarter(held, mixed)), r, COARSE, drained)
 
             def quarters(mixed, carry):
-                emit(held, mixed, target, *quarter(held, mixed), cos_half, sin_half, SEND_ORDER, lambda o: o, (0,))
+                emit(held, mixed, target, *quarter(held, mixed), cos_half, sin_half, size, SEND_ORDER, lambda o: o, (0,))
                 return carry
 
             lax.fori_loop(0, 2, quarters, 0)
@@ -314,29 +323,34 @@
         return carry
 
     lax.fori_loop(0, LAYERS // 2 - 2, layer_pair, 0)
-    run_layer(LAYERS - 1, False, 7, 7)
+    run_layer(LAYERS - 1, False, 7, 7, FINE)
 
     cos_half, sin_half = half_angle(LAYERS - 1)
     energy_part[...] = jnp.zeros((8, LANES), jnp.float32)
 
     def final_half(a, carry):
-        def slots(r, carry):
+        def message(i, carry):
             for b in range(2):
-                wait_all(recv, recv_sem, (0, a, b, r), 7)
-            old = [[recv[0, a, b, r, o, c] for b in range(2) for o in range(8)] for c in range(2)]
-            re, im = rotate(*old, cos_half, sin_half)
-            total = energy_part[...]
-            for b in range(2):
-                for o in range(8):
-                    at = (block(o), a, b, rows_of(r))
-                    x, y = re[b * 8 + o], im[b * 8 + o]
-                    out_re[at] = x
-                    out_im[at] = y
-                    total = total + cost[at] * (x * x + y * y)
-            energy_part[...] = total
-            return carry
-
-        lax.fori_loop(0, 8, slots, 0)
+                wait_all(recv, recv_sem, (0, a, b), i * FINE, FINE, 7)
+
+            def slots(r, carry):
+                old = [[recv[0, a, b, o, r, c] for b in range(2) for o in range(8)] for c in range(2)]
+                re, im = rotate(*old, cos_half, sin_half)
+                total = energy_part[...]
+                for b in range(2):
+                    for o in range(8):
+                        at = (block(o), a, b, rows_of(r))
+                        x, y = re[b * 8 + o], im[b * 8 + o]
+                        out_re[at] = x
+                        out_im[at] = y
+                        total = total + cost[at] * (x * x + y * y)
+                energy_part[...] = total
+                return carry
+
+            lax.fori_loop(i * FINE, (i + 1) * FINE, slots, 0)
+            return carry
+
+        lax.fori_loop(0, 8 // FINE, message, 0)
         return carry
 
     lax.fori_loop(0, 2, final_half, 0)
@@ -349,8 +363,9 @@
     for par in range(2):
         for a in range(2):
             for b in range(2):
-                for r in range(8):
-                    wait_all(send, send_sem, (par, a, b, r), 7)
+                size = COARSE if par else FINE
+                for r in range(0, 8, size):
+                    wait_all(send, send_sem, (par, a, b), r, size, 7)
     for a in range(2):
         for sub in range(PAIRS):
             wait_bytes(cost.at[:, a, :, pl.ds(sub * 16, 16)], near_send.at[a, sub])

time: 197 us -> 197 us (level)
  no operation moved by 1% of the time
where the time goes in v12:
time: 197 us
  Pallas kernels  197 us (100%)
    pallas_call x1, Pallas kernels, device_body(): pl.pallas_call(kernel, out_shape=(pltpu.VMEM((8, 1, LANES), f32), pltpu.V...  195 us

profile of v12, /device:TPU:0, one launch (start us, length us, event | category | flops | bytes accessed | tf_op | source)
XLA Modules:
  0.0 197.4 jit_solution(9368918027179194713)
XLA Ops:
  0.6 195.4 %qaoa.1 = (f32[8,1,128]{2,1,0:T(1,128)S(1)}, f32[8,2,2,64,128]{4,3,2,1,0:T(8,128)S(1)}, f32[8,2,2,64,128]{4,3,2,1,0:T(8,128)S(1)}) custom-call(f32[8,2,2,64,128]{4,3,2,1,0:T(8,128)} %bitcast.3, f32[8]{0:T(128)} %gammas_hbm.1, f32[8]{0:T(128)} %betas_hbm.1), custom_call_target="tpu_custom_call" | custom-call | tf_op jit(solution)/shard_map/qaoa/pallas_call | solution.py:403
  196.0 1.4 write_out.1

commit v13 on v9

--- a/solution.py
+++ b/solution.py
@@ -131,7 +131,13 @@
             rows_in[...], matrix[...],
             precision=lax.Precision.HIGHEST, preferred_element_type=jnp.float32)
 
-    def emit(held, mixed, target, a, b, cos_half, sin_half, order, route, local):
+    def send_parts(target, a, b, subs, order, route):
+        for sub in subs:
+            at = (target, a, b, sub)
+            for o in order:
+                remote(send.at[(*at, o)], recv.at[(*at, o)], send_sem.at[at], recv_sem.at[at], route(o))
+
+    def emit(held, mixed, target, a, b, cos_half, sin_half, local):
         def across(o, buffer):
             def part(r, c):
                 at = pl.multiple_of((mixed * 8 + o) * 16 + (r % 2) * 8, 8)
@@ -152,11 +158,6 @@
         lax.fori_loop(1, 8, body, 0)
         for o in local:
             across(o, recv)
-        for sub in range(SUB):
-            at = (target, a, b, sub)
-            for o in order:
-                remote(send.at[(*at, o)], recv.at[(*at, o)], send_sem.at[at], recv_sem.at[at], route(o))
-
     def first_layer():
         def sub_rows(sub):
             return pl.ds(pl.multiple_of(sub * 8 * PER_SUB, 8), 8 * PER_SUB)
@@ -234,8 +235,8 @@
         def quarters(b, carry):
             for a in range(2):
                 bit = NEAR[a]
-                emit(a, b, 1, a, b, cos_half, sin_half,
-                     [o for o in (3, 6, 7, 1, 4, 5, 2) if o & ~bit], lambda o: o & ~bit, (0, bit))
+                emit(a, b, 1, a, b, cos_half, sin_half, (0, bit))
+                send_parts(1, a, b, range(SUB), [o for o in (3, 6, 7, 1, 4, 5, 2) if o & ~bit], lambda o: o & ~bit)
             return carry
 
         lax.fori_loop(0, 2, quarters, 0)
@@ -296,11 +297,23 @@
                     for sub in range(SUB):
                         wait_all(send, send_sem, (target, *quarter(held, mixed), sub), drained)
 
-            def quarters(mixed, carry):
-                emit(held, mixed, target, *quarter(held, mixed), cos_half, sin_half, SEND_ORDER, lambda o: o, (0,))
-                return carry
-
-            lax.fori_loop(0, 2, quarters, 0)
+            def parts(held, mixed, subs):
+                send_parts(target, *quarter(held, mixed), subs, SEND_ORDER, lambda o: o)
+
+            emit(held, 0, target, *quarter(held, 0), cos_half, sin_half, (0,))
+            parts(held, 0, range(SUB))
+
+            @pl.when(held == 1)
+            def _():
+                parts(0, 1, range(SUB // 2, SUB))
+
+            emit(held, 1, target, *quarter(held, 1), cos_half, sin_half, (0,))
+            parts(held, 1, range(SUB // 2))
+
+            @pl.when(held == 1)
+            def _():
+                parts(1, 1, range(SUB // 2, SUB))
+
             return carry
 
         lax.fori_loop(0, 2, half, 0)

time: 197 us -> 197 us (level)
  no operation moved by 1% of the time
where the time goes in v13:
time: 197 us
  Pallas kernels  196 us (99%)
    pallas_call x1, Pallas kernels, device_body(): pl.pallas_call(kernel, out_shape=(pltpu.VMEM((8, 1, LANES), f32), pltpu.V...  195 us

profile of v13, /device:TPU:0, one launch (start us, length us, event | category | flops | bytes accessed | tf_op | source)
XLA Modules:
  0.0 196.6 jit_solution(11851322260908105474)
XLA Ops:
  0.6 194.7 %qaoa.1 = (f32[8,1,128]{2,1,0:T(1,128)S(1)}, f32[8,2,2,64,128]{4,3,2,1,0:T(8,128)S(1)}, f32[8,2,2,64,128]{4,3,2,1,0:T(8,128)S(1)}) custom-call(f32[8,2,2,64,128]{4,3,2,1,0:T(8,128)} %bitcast.3, f32[8]{0:T(128)} %gammas_hbm.1, f32[8]{0:T(128)} %betas_hbm.1), custom_call_target="tpu_custom_call" | custom-call | tf_op jit(solution)/shard_map/qaoa/pallas_call | solution.py:409
  195.3 1.4 write_out.1

commit v14 on v9

--- a/solution.py
+++ b/solution.py
@@ -9,7 +9,6 @@
 LAYERS = 8
 SUB = 4
 PER_SUB = 8 // SUB
-SEND_ORDER = (5, 7, 4, 6, 1, 3, 2)
 NEAR = (4, 1)
 
 
@@ -154,6 +153,18 @@
             across(o, recv)
         for sub in range(SUB):
             at = (target, a, b, sub)
+            if route is None:
+                y, core, x = bits
+                for x_step, y_step in ((1, 1), (1, 0), (0, 1)):
+                    for turn in (core, 1 - core):
+                        o = 4 * x_step + 2 * turn + y_step
+                        pltpu.make_async_remote_copy(
+                            src_ref=send.at[(*at, o)], dst_ref=recv.at[(*at, o)],
+                            send_sem=send_sem.at[at], recv_sem=recv_sem.at[at],
+                            device_id={'qy': (y + y_step) % 2, 'qx': (x + x_step) % 2 * 2 + (core + turn) % 2},
+                            device_id_type=pl.DeviceIdType.MESH).start()
+                remote(send.at[(*at, 2)], recv.at[(*at, 2)], send_sem.at[at], recv_sem.at[at], 2)
+                continue
             for o in order:
                 remote(send.at[(*at, o)], recv.at[(*at, o)], send_sem.at[at], recv_sem.at[at], route(o))
 
@@ -297,7 +308,7 @@
                         wait_all(send, send_sem, (target, *quarter(held, mixed), sub), drained)
 
             def quarters(mixed, carry):
-                emit(held, mixed, target, *quarter(held, mixed), cos_half, sin_half, SEND_ORDER, lambda o: o, (0,))
+                emit(held, mixed, target, *quarter(held, mixed), cos_half, sin_half, (), None, (0,))
                 return carry
 
             lax.fori_loop(0, 2, quarters, 0)

time: 197 us -> 197 us (level)
  no operation moved by 1% of the time
where the time goes in v14:
time: 197 us
  Pallas kernels  196 us (99%)
    pallas_call x1, Pallas kernels, device_body(): pl.pallas_call(kernel, out_shape=(pltpu.VMEM((8, 1, LANES), f32), pltpu.V...  195 us

profile of v14, /device:TPU:0, one launch (start us, length us, event | category | flops | bytes accessed | tf_op | source)
XLA Modules:
  0.0 196.6 jit_solution(7564410843905090453)
XLA Ops:
  0.6 194.7 %qaoa.1 = (f32[8,1,128]{2,1,0:T(1,128)S(1)}, f32[8,2,2,64,128]{4,3,2,1,0:T(8,128)S(1)}, f32[8,2,2,64,128]{4,3,2,1,0:T(8,128)S(1)}) custom-call(f32[8,2,2,64,128]{4,3,2,1,0:T(8,128)} %bitcast.3, f32[8]{0:T(128)} %gammas_hbm.1, f32[8]{0:T(128)} %betas_hbm.1), custom_call_target="tpu_custom_call" | custom-call | tf_op jit(solution)/shard_map/qaoa/pallas_call | solution.py:407
  195.3 1.4 write_out.1

commit v15 on v12

--- a/solution.py
+++ b/solution.py
@@ -7,8 +7,8 @@
 
 LANES = 128
 LAYERS = 8
-COARSE = 4
-FINE = 2
+FIRST = 2
+REST = 1
 PAIRS = 4
 SEND_ORDER = (5, 7, 4, 6, 1, 3, 2)
 NEAR = (4, 1)
@@ -235,7 +235,7 @@
         def quarters(b, carry):
             for a in range(2):
                 bit = NEAR[a]
-                emit(a, b, 1, a, b, cos_half, sin_half, COARSE,
+                emit(a, b, 1, a, b, cos_half, sin_half, FIRST,
                      [o for o in (3, 6, 7, 1, 4, 5, 2) if o & ~bit], lambda o: o & ~bit, (0, bit))
             return carry
 
@@ -245,7 +245,7 @@
             cost_swap[NEAR[a], a] = cost_near[block(0), a]
         wait_bytes(cost_swap.at[pl.ds(0, 6)], cost_recv)
 
-    def run_layer(layer, odd, arrived, drained, size=COARSE):
+    def run_layer(layer, odd, arrived, drained, size_in=REST, size_drained=REST):
         source, target = (0, 1) if odd else (1, 0)
 
         def quarter(held, mixed):
@@ -268,7 +268,11 @@
 
             lax.fori_loop(0, 8, trig, 0)
 
-            def block_step(sub):
+            def block_step(sub, carry):
+                for i in range(0, 2, size_in):
+                    for mixed in range(2):
+                        wait_all(recv, recv_sem, (source, *quarter(held, mixed)), 2 * sub + i, size_in, arrived)
+
                 def slots(i, carry):
                     r = 2 * sub + i
                     cos_phase = [cos_buf[held, o, rows_of(r), :] for o in range(16)]
@@ -285,27 +289,17 @@
 
                 lax.fori_loop(0, 2, slots, 0)
                 lanes(held, sub)
-
-            def message(i, carry):
-                for mixed in range(2):
-                    wait_all(recv, recv_sem, (source, *quarter(held, mixed)), i * COARSE, COARSE, arrived)
-
-                def blocks(k, carry):
-                    block_step(i * (COARSE // 2) + k)
-                    return carry
-
-                lax.fori_loop(0, COARSE // 2, blocks, 0)
                 return carry
 
-            lax.fori_loop(0, 8 // COARSE, message, 0)
+            lax.fori_loop(0, PAIRS, block_step, 0)
 
             if drained:
                 for mixed in range(2):
-                    for r in range(0, 8, COARSE):
-                        wait_all(send, send_sem, (target, *quarter(held, mixed)), r, COARSE, drained)
+                    for r in range(0, 8, size_drained):
+                        wait_all(send, send_sem, (target, *quarter(held, mixed)), r, size_drained, drained)
 
             def quarters(mixed, carry):
-                emit(held, mixed, target, *quarter(held, mixed), cos_half, sin_half, size, SEND_ORDER, lambda o: o, (0,))
+                emit(held, mixed, target, *quarter(held, mixed), cos_half, sin_half, REST, SEND_ORDER, lambda o: o, (0,))
                 return carry
 
             lax.fori_loop(0, 2, quarters, 0)
@@ -314,8 +308,8 @@
         lax.fori_loop(0, 2, half, 0)
 
     first_layer()
-    run_layer(1, False, 6, 0)
-    run_layer(2, True, 7, 6)
+    run_layer(1, False, 6, 0, size_in=FIRST)
+    run_layer(2, True, 7, 6, size_drained=FIRST)
 
     def layer_pair(i, carry):
         run_layer(2 * i + 3, False, 7, 7)
@@ -323,7 +317,7 @@
         return carry
 
     lax.fori_loop(0, LAYERS // 2 - 2, layer_pair, 0)
-    run_layer(LAYERS - 1, False, 7, 7, FINE)
+    run_layer(LAYERS - 1, False, 7, 7)
 
     cos_half, sin_half = half_angle(LAYERS - 1)
     energy_part[...] = jnp.zeros((8, LANES), jnp.float32)
@@ -331,7 +325,7 @@
     def final_half(a, carry):
         def message(i, carry):
             for b in range(2):
-                wait_all(recv, recv_sem, (0, a, b), i * FINE, FINE, 7)
+                wait_all(recv, recv_sem, (0, a, b), i * REST, REST, 7)
 
             def slots(r, carry):
                 old = [[recv[0, a, b, o, r, c] for b in range(2) for o in range(8)] for c in range(2)]
@@ -347,10 +341,10 @@
                 energy_part[...] = total
                 return carry
 
-            lax.fori_loop(i * FINE, (i + 1) * FINE, slots, 0)
-            return carry
-
-        lax.fori_loop(0, 8 // FINE, message, 0)
+            lax.fori_loop(i * REST, (i + 1) * REST, slots, 0)
+            return carry
+
+        lax.fori_loop(0, 8 // REST, message, 0)
         return carry
 
     lax.fori_loop(0, 2, final_half, 0)
@@ -363,9 +357,8 @@
     for par in range(2):
         for a in range(2):
             for b in range(2):
-                size = COARSE if par else FINE
-                for r in range(0, 8, size):
-                    wait_all(send, send_sem, (par, a, b), r, size, 7)
+                for r in range(0, 8, REST):
+                    wait_all(send, send_sem, (par, a, b), r, REST, 7)
     for a in range(2):
         for sub in range(PAIRS):
             wait_bytes(cost.at[:, a, :, pl.ds(sub * 16, 16)], near_send.at[a, sub])

time: 197 us -> 197 us (level)
  no operation moved by 1% of the time
where the time goes in v15:
time: 197 us
  Pallas kernels  197 us (100%)
    pallas_call x1, Pallas kernels, device_body(): pl.pallas_call(kernel, out_shape=(pltpu.VMEM((8, 1, LANES), f32), pltpu.V...  195 us

profile of v15, /device:TPU:0, one launch (start us, length us, event | category | flops | bytes accessed | tf_op | source)
XLA Modules:
  0.0 197.2 jit_solution(3483114799464314118)
XLA Ops:
  0.6 195.2 %qaoa.1 = (f32[8,1,128]{2,1,0:T(1,128)S(1)}, f32[8,2,2,64,128]{4,3,2,1,0:T(8,128)S(1)}, f32[8,2,2,64,128]{4,3,2,1,0:T(8,128)S(1)}) custom-call(f32[8,2,2,64,128]{4,3,2,1,0:T(8,128)} %bitcast.3, f32[8]{0:T(128)} %gammas_hbm.1, f32[8]{0:T(128)} %betas_hbm.1), custom_call_target="tpu_custom_call" | custom-call | tf_op jit(solution)/shard_map/qaoa/pallas_call | solution.py:396
  195.9 1.4 write_out.1

commit v16 on v9

--- a/solution.py
+++ b/solution.py
@@ -63,6 +63,33 @@
            cost, cost_near, cost_swap, recv, send, work, cos_buf, sin_buf, cos_near, sin_near,
            rows_in, matrix, energy_part, energy_row, gammas, betas, angle_in, near_in, cost_in, near_send, near_recv, cost_send, cost_recv,
            send_sem, recv_sem, e_send, e_recv):
+    qx = lax.axis_index('qx')
+    qy = lax.axis_index('qy')
+    bits = (qy, qx % 2, qx // 2)
+
+    def flipped(offset):
+        return [1 - bit if (offset >> i) & 1 else bit for i, bit in enumerate(bits)]
+
+    def block(offset):
+        y, core, x = flipped(offset)
+        return (x * 2 + core) * 2 + y
+
+    def peer(offset):
+        y, core, x = flipped(offset)
+        return {'qy': y, 'qx': x * 2 + core}
+
+    def remote(source, target, send_at, recv_at, offset):
+        pltpu.make_async_remote_copy(
+            src_ref=source, dst_ref=target, send_sem=send_at, recv_sem=recv_at,
+            device_id=peer(offset), device_id_type=pl.DeviceIdType.MESH).start()
+
+    barrier = pltpu.get_barrier_semaphore()
+
+    def signal_next(sem):
+        for offset in (4, 1, 2):
+            pl.semaphore_signal(sem, inc=1, device_id=peer(offset), device_id_type=pl.DeviceIdType.MESH)
+
+    signal_next(barrier)
     loads = [pltpu.make_async_copy(cost_hbm.at[:, :, :, pl.ds(sub * 8 * PER_SUB, 8 * PER_SUB)],
                                    cost.at[:, :, :, pl.ds(sub * 8 * PER_SUB, 8 * PER_SUB)], cost_in.at[sub])
              for sub in range(SUB)]
@@ -72,32 +99,6 @@
                    pltpu.make_async_copy(betas_hbm, betas, angle_in.at[1])]
     for load in angle_loads:
         load.start()
-    qx = lax.axis_index('qx')
-    qy = lax.axis_index('qy')
-    bits = (qy, qx % 2, qx // 2)
-
-    def flipped(offset):
-        return [1 - bit if (offset >> i) & 1 else bit for i, bit in enumerate(bits)]
-
-    def block(offset):
-        y, core, x = flipped(offset)
-        return (x * 2 + core) * 2 + y
-
-    def peer(offset):
-        y, core, x = flipped(offset)
-        return {'qy': y, 'qx': x * 2 + core}
-
-    def remote(source, target, send_at, recv_at, offset):
-        pltpu.make_async_remote_copy(
-            src_ref=source, dst_ref=target, send_sem=send_at, recv_sem=recv_at,
-            device_id=peer(offset), device_id_type=pl.DeviceIdType.MESH).start()
-
-    barrier = pltpu.get_barrier_semaphore()
-    def signal_next(sem):
-        for offset in (4, 1, 2):
-            pl.semaphore_signal(sem, inc=1, device_id=peer(offset), device_id_type=pl.DeviceIdType.MESH)
-
-    signal_next(barrier)
     pl.semaphore_wait(barrier, 3)
 
     def half_angle(layer):
@@ -120,16 +121,15 @@
         matrix[LANES:, 0:LANES] = -imag
         matrix[LANES:, LANES:] = real
 
-    def put_rows(i, re, im):
+    def put_rows(i, re, im, base=0):
         for o in range(16):
-            at = pl.multiple_of(o * 16 + i * 8, 8)
+            at = pl.multiple_of(base + o * 16 + i * 8, 8)
             rows_in[pl.ds(at, 8), 0:LANES] = re[o]
             rows_in[pl.ds(at, 8), LANES:] = im[o]
 
-    def lanes(a_held, at):
-        work[a_held, at] = lax.dot(
-            rows_in[...], matrix[...],
-            precision=lax.Precision.HIGHEST, preferred_element_type=jnp.float32)
+    def lanes(count):
+        return lax.dot(rows_in[0:count, :], matrix[...],
+                       precision=lax.Precision.HIGHEST, preferred_element_type=jnp.float32)
 
     def emit(held, mixed, target, a, b, cos_half, sin_half, order, route, local):
         def across(o, buffer):
@@ -222,11 +222,13 @@
                                 im[slot] = -(cos_half * sin_at(here)) - sin_half * cos_at(there)
                     re, im = rotate(re, im, cos_half, sin_half, [step for step in (1, 2, 4, 8) if step != bit])
                     re, im = sublane_rotate(re, im, cos_half, sin_half)
-                    put_rows(i, re, im)
+                    put_rows(i, re, im, a * 2 * LANES)
                     return carry
 
                 lax.fori_loop(0, PER_SUB, slots, 0)
-                lanes(a, sub)
+            rows = lanes(4 * LANES)
+            for a in range(2):
+                work[a, sub] = rows[a * 2 * LANES:(a + 1) * 2 * LANES]
             return carry
 
         lax.fori_loop(0, SUB, sub_step, 0)
@@ -286,7 +288,7 @@
                     return carry
 
                 lax.fori_loop(0, PER_SUB, slots, 0)
-                lanes(held, sub)
+                work[held, sub] = lanes(2 * LANES)
                 return carry
 
             lax.fori_loop(0, SUB, sub_step, 0)
@@ -404,7 +406,7 @@
                 pltpu.VMEM((2, 4, 2 * LANES, 2 * LANES), f32),
                 pltpu.VMEM((2, 16, 64, LANES), f32), pltpu.VMEM((2, 16, 64, LANES), f32),
                 pltpu.VMEM((16, 8, LANES), f32), pltpu.VMEM((16, 8, LANES), f32),
-                pltpu.VMEM((2 * LANES, 2 * LANES), f32), pltpu.VMEM((2 * LANES, 2 * LANES), f32),
+                pltpu.VMEM((4 * LANES, 2 * LANES), f32), pltpu.VMEM((2 * LANES, 2 * LANES), f32),
                 pltpu.VMEM((8, LANES), f32), pltpu.VMEM((1, LANES), f32),
                 pltpu.SMEM((LAYERS,), f32), pltpu.SMEM((LAYERS,), f32), dma((2,)), pltpu.SemaphoreType.REGULAR((2,)),
                 dma((SUB,)), dma((2, SUB)), dma((2, SUB)), dma, dma,

time: 197 us -> 197 us (level)
  no operation moved by 1% of the time
where the time goes in v16:
time: 197 us
  Pallas kernels  196 us (99%)
    pallas_call x1, Pallas kernels, device_body(): pl.pallas_call(kernel, out_shape=(pltpu.VMEM((8, 1, LANES), f32), pltpu.V...  195 us

profile of v16, /device:TPU:0, one launch (start us, length us, event | category | flops | bytes accessed | tf_op | source)
XLA Modules:
  0.0 196.6 jit_solution(1450193396484230724)
XLA Ops:
  0.6 194.6 %qaoa.1 = (f32[8,1,128]{2,1,0:T(1,128)S(1)}, f32[8,2,2,64,128]{4,3,2,1,0:T(8,128)S(1)}, f32[8,2,2,64,128]{4,3,2,1,0:T(8,128)S(1)}) custom-call(f32[8,2,2,64,128]{4,3,2,1,0:T(8,128)} %bitcast.3, f32[8]{0:T(128)} %gammas_hbm.1, f32[8]{0:T(128)} %betas_hbm.1), custom_call_target="tpu_custom_call" | custom-call | tf_op jit(solution)/shard_map/qaoa/pallas_call | solution.py:398
  195.3 1.4 write_out.1

commit v17 on v16

--- a/solution.py
+++ b/solution.py
@@ -353,18 +353,22 @@
 
     me = block(0)
     energy_row[...] = jnp.sum(energy_part[...], axis=0, keepdims=True)
-    for offset in range(1, 8):
-        remote(energy_row, energy_all.at[me], e_send.at[offset], e_recv.at[offset], offset)
     energy_all[me] = energy_row[...]
-    for par in range(2):
+
+    def drain(par):
         for a in range(2):
             for b in range(2):
                 for sub in range(SUB):
                     wait_all(send, send_sem, (par, a, b, sub), 7)
+
+    drain(1)
     for a in range(2):
         for sub in range(SUB):
             wait_bytes(cost.at[:, a, :, pl.ds(sub * 8 * PER_SUB, 8 * PER_SUB)], near_send.at[a, sub])
     wait_bytes(cost_swap.at[pl.ds(0, 6)], cost_send)
+    for offset in range(1, 8):
+        remote(energy_row, energy_all.at[me], e_send.at[offset], e_recv.at[offset], offset)
+    drain(0)
     for offset in range(1, 8):
         wait_bytes(energy_row, e_send.at[offset])
         wait_bytes(energy_row, e_recv.at[offset])

time: 197 us -> 197 us (level)
  no operation moved by 1% of the time
where the time goes in v17:
time: 197 us
  Pallas kernels  196 us (99%)
    pallas_call x1, Pallas kernels, device_body(): pl.pallas_call(kernel, out_shape=(pltpu.VMEM((8, 1, LANES), f32), pltpu.V...  195 us

profile of v17, /device:TPU:0, one launch (start us, length us, event | category | flops | bytes accessed | tf_op | source)
XLA Modules:
  0.0 196.7 jit_solution(1289275453866704510)
XLA Ops:
  0.6 194.7 %qaoa.1 = (f32[8,1,128]{2,1,0:T(1,128)S(1)}, f32[8,2,2,64,128]{4,3,2,1,0:T(8,128)S(1)}, f32[8,2,2,64,128]{4,3,2,1,0:T(8,128)S(1)}) custom-call(f32[8,2,2,64,128]{4,3,2,1,0:T(8,128)} %bitcast.3, f32[8]{0:T(128)} %gammas_hbm.1, f32[8]{0:T(128)} %betas_hbm.1), custom_call_target="tpu_custom_call" | custom-call | tf_op jit(solution)/shard_map/qaoa/pallas_call | solution.py:402
  195.3 1.4 write_out.1

commit v18 on v17

--- a/solution.py
+++ b/solution.py
@@ -59,6 +59,9 @@
     return real, imag
 
 
+ENERGY_ORDER = (7, 5, 6, 4, 3, 1, 2)
+
+
 def kernel(cost_hbm, gammas_hbm, betas_hbm, energy_all, out_re, out_im,
            cost, cost_near, cost_swap, recv, send, work, cos_buf, sin_buf, cos_near, sin_near,
            rows_in, matrix, energy_part, energy_row, gammas, betas, angle_in, near_in, cost_in, near_send, near_recv, cost_send, cost_recv,
@@ -111,6 +114,9 @@
     def wait_all(buffer, sem, at, count):
         wait_bytes(buffer.at[(*at, pl.ds(0, count))], sem.at[at])
 
+    def wait_last(buffer, sem, a, b, part):
+        wait_bytes(buffer.at[0, a, b, 0, pl.ds(0, 7), :, pl.ds(0, 8)], sem.at[0, a, b, SUB - 1 + part])
+
     def rows_of(r):
         return pl.ds(pl.multiple_of(r * 8, 8), 8)
 
@@ -131,7 +137,7 @@
         return lax.dot(rows_in[0:count, :], matrix[...],
                        precision=lax.Precision.HIGHEST, preferred_element_type=jnp.float32)
 
-    def emit(held, mixed, target, a, b, cos_half, sin_half, order, route, local):
+    def emit(held, mixed, target, a, b, cos_half, sin_half, order, route, local, last=False):
         def across(o, buffer):
             def part(r, c):
                 at = pl.multiple_of((mixed * 8 + o) * 16 + (r % 2) * 8, 8)
@@ -152,10 +158,16 @@
         lax.fori_loop(1, 8, body, 0)
         for o in local:
             across(o, recv)
-        for sub in range(SUB):
+        for sub in range(SUB - last):
             at = (target, a, b, sub)
             for o in order:
                 remote(send.at[(*at, o)], recv.at[(*at, o)], send_sem.at[at], recv_sem.at[at], route(o))
+        if last:
+            for part in range(2):
+                sem_at = (target, a, b, SUB - 1 + part)
+                for o in order:
+                    at = (target, a, b, SUB - 1, o, slice(None), pl.ds(8 * part, 8))
+                    remote(send.at[at], recv.at[at], send_sem.at[sem_at], recv_sem.at[sem_at], route(o))
 
     def first_layer():
         def sub_rows(sub):
@@ -246,7 +258,7 @@
             cost_swap[NEAR[a], a] = cost_near[block(0), a]
         wait_bytes(cost_swap.at[pl.ds(0, 6)], cost_recv)
 
-    def run_layer(layer, odd, arrived, drained):
+    def run_layer(layer, odd, arrived, drained, last=False):
         source, target = (0, 1) if odd else (1, 0)
 
         def quarter(held, mixed):
@@ -299,7 +311,7 @@
                         wait_all(send, send_sem, (target, *quarter(held, mixed), sub), drained)
 
             def quarters(mixed, carry):
-                emit(held, mixed, target, *quarter(held, mixed), cos_half, sin_half, SEND_ORDER, lambda o: o, (0,))
+                emit(held, mixed, target, *quarter(held, mixed), cos_half, sin_half, SEND_ORDER, lambda o: o, (0,), last)
                 return carry
 
             lax.fori_loop(0, 2, quarters, 0)
@@ -317,36 +329,46 @@
         return carry
 
     lax.fori_loop(0, LAYERS // 2 - 2, layer_pair, 0)
-    run_layer(LAYERS - 1, False, 7, 7)
+    run_layer(LAYERS - 1, False, 7, 7, True)
 
     cos_half, sin_half = half_angle(LAYERS - 1)
     energy_part[...] = jnp.zeros((8, LANES), jnp.float32)
 
     def final_half(a, carry):
+        def slots(sub, i):
+            r = sub * PER_SUB + i
+            old = [[recv[0, a, b, sub, o, c, rows_of(i), :] for b in range(2) for o in range(8)]
+                   for c in range(2)]
+            re, im = rotate(*old, cos_half, sin_half)
+            total = energy_part[...]
+            for b in range(2):
+                for o in range(8):
+                    at = (block(o), a, b, rows_of(r))
+                    x, y = re[b * 8 + o], im[b * 8 + o]
+                    out_re[at] = x
+                    out_im[at] = y
+                    total = total + cost[at] * (x * x + y * y)
+            energy_part[...] = total
+
         def final_sub(sub, carry):
             for b in range(2):
                 wait_all(recv, recv_sem, (0, a, b, sub), 7)
 
-            def slots(i, carry):
-                r = sub * PER_SUB + i
-                old = [[recv[0, a, b, sub, o, c, rows_of(i), :] for b in range(2) for o in range(8)]
-                       for c in range(2)]
-                re, im = rotate(*old, cos_half, sin_half)
-                total = energy_part[...]
-                for b in range(2):
-                    for o in range(8):
-                        at = (block(o), a, b, rows_of(r))
-                        x, y = re[b * 8 + o], im[b * 8 + o]
-                        out_re[at] = x
-                        out_im[at] = y
-                        total = total + cost[at] * (x * x + y * y)
-                energy_part[...] = total
+            def body(i, carry):
+                slots(sub, i)
                 return carry
 
-            lax.fori_loop(0, PER_SUB, slots, 0)
-            return carry
-
-        lax.fori_loop(0, SUB, final_sub, 0)
+            lax.fori_loop(0, PER_SUB, body, 0)
+            return carry
+
+        def final_part(part, carry):
+            for b in range(2):
+                wait_last(recv, recv_sem, a, b, part)
+            slots(SUB - 1, part)
+            return carry
+
+        lax.fori_loop(0, SUB - 1, final_sub, 0)
+        lax.fori_loop(0, 2, final_part, 0)
         return carry
 
     lax.fori_loop(0, 2, final_half, 0)
@@ -358,15 +380,18 @@
     def drain(par):
         for a in range(2):
             for b in range(2):
-                for sub in range(SUB):
+                for sub in range(SUB if par else SUB - 1):
                     wait_all(send, send_sem, (par, a, b, sub), 7)
+                if not par:
+                    wait_last(send, send_sem, a, b, 0)
+                    wait_last(send, send_sem, a, b, 1)
 
     drain(1)
     for a in range(2):
         for sub in range(SUB):
             wait_bytes(cost.at[:, a, :, pl.ds(sub * 8 * PER_SUB, 8 * PER_SUB)], near_send.at[a, sub])
     wait_bytes(cost_swap.at[pl.ds(0, 6)], cost_send)
-    for offset in range(1, 8):
+    for offset in ENERGY_ORDER:
         remote(energy_row, energy_all.at[me], e_send.at[offset], e_recv.at[offset], offset)
     drain(0)
     for offset in range(1, 8):
@@ -414,7 +439,7 @@
                 pltpu.VMEM((8, LANES), f32), pltpu.VMEM((1, LANES), f32),
                 pltpu.SMEM((LAYERS,), f32), pltpu.SMEM((LAYERS,), f32), dma((2,)), pltpu.SemaphoreType.REGULAR((2,)),
                 dma((SUB,)), dma((2, SUB)), dma((2, SUB)), dma, dma,
-                dma((2, 2, 2, SUB)), dma((2, 2, 2, SUB)),
+                dma((2, 2, 2, SUB + 1)), dma((2, 2, 2, SUB + 1)),
                 dma((8,)), dma((8,)),
             ],
             compiler_params=pltpu.CompilerParams(collective_id=0, has_side_effects=True),

time: 197 us -> 197 us (level)
  no operation moved by 1% of the time
where the time goes in v18:
time: 197 us
  Pallas kernels  196 us (99%)
    pallas_call x1, Pallas kernels, device_body(): pl.pallas_call(kernel, out_shape=(pltpu.VMEM((8, 1, LANES), f32), pltpu.V...  195 us

profile of v18, /device:TPU:0, one launch (start us, length us, event | category | flops | bytes accessed | tf_op | source)
XLA Modules:
  0.0 196.9 jit_solution(3832894610300762717)
XLA Ops:
  0.6 194.9 %qaoa.1 = (f32[8,1,128]{2,1,0:T(1,128)S(1)}, f32[8,2,2,64,128]{4,3,2,1,0:T(8,128)S(1)}, f32[8,2,2,64,128]{4,3,2,1,0:T(8,128)S(1)}) custom-call(f32[8,2,2,64,128]{4,3,2,1,0:T(8,128)} %bitcast.3, f32[8]{0:T(128)} %gammas_hbm.1, f32[8]{0:T(128)} %betas_hbm.1), custom_call_target="tpu_custom_call" | custom-call | tf_op jit(solution)/shard_map/qaoa/pallas_call | solution.py:427
  195.5 1.4 write_out.1

commit v19 on v17

--- a/solution.py
+++ b/solution.py
@@ -361,29 +361,30 @@
                 for sub in range(SUB):
                     wait_all(send, send_sem, (par, a, b, sub), 7)
 
-    drain(1)
     for a in range(2):
         for sub in range(SUB):
             wait_bytes(cost.at[:, a, :, pl.ds(sub * 8 * PER_SUB, 8 * PER_SUB)], near_send.at[a, sub])
     wait_bytes(cost_swap.at[pl.ds(0, 6)], cost_send)
-    for offset in range(1, 8):
+    for offset in (7, 5, 6, 4, 3, 1, 2):
         remote(energy_row, energy_all.at[me], e_send.at[offset], e_recv.at[offset], offset)
     drain(0)
+    drain(1)
     for offset in range(1, 8):
         wait_bytes(energy_row, e_send.at[offset])
         wait_bytes(energy_row, e_recv.at[offset])
 
 
 def write_out(energy_all, in_re, in_im, energy, out_re, out_im, value, sem):
-    copies = [pltpu.make_async_copy(in_re, out_re, sem.at[0]), pltpu.make_async_copy(in_im, out_im, sem.at[1])]
+    copies = [pltpu.make_async_copy(source.at[pl.ds(4 * i, 4)], result.at[pl.ds(4 * i, 4)], sem.at[2 * c + i])
+              for i in range(2) for c, (source, result) in enumerate(((in_re, out_re), (in_im, out_im)))]
     for copy in copies:
         copy.start()
     total = energy_all[0]
     for i in range(1, 8):
         total = total + energy_all[i]
     value[0] = jnp.sum(total) * (1.0 / (1 << 21))
-    copies.append(pltpu.make_async_copy(value, energy, sem.at[2]))
-    copies[2].start()
+    copies.append(pltpu.make_async_copy(value, energy, sem.at[4]))
+    copies[4].start()
     for copy in copies:
         copy.wait()
 
@@ -426,7 +427,7 @@
                        jax.ShapeDtypeStruct(shape, f32), jax.ShapeDtypeStruct(shape, f32)),
             in_specs=[vmem, vmem, vmem],
             out_specs=(hbm, hbm, hbm),
-            scratch_shapes=[pltpu.SMEM((1,), f32), dma((3,))],
+            scratch_shapes=[pltpu.SMEM((1,), f32), dma((5,))],
             name='write_out',
         )(*[pltpu.with_memory_space_constraint(value, pltpu.VMEM) for value in results])
         return energy, state_re.reshape(local_len), state_im.reshape(local_len)

time: 197 us -> 197 us (level)
  no operation moved by 1% of the time
where the time goes in v19:
time: 197 us
  Pallas kernels  196 us (99%)
    pallas_call x1, Pallas kernels, device_body(): pl.pallas_call(kernel, out_shape=(pltpu.VMEM((8, 1, LANES), f32), pltpu.V...  195 us

profile of v19, /device:TPU:0, one launch (start us, length us, event | category | flops | bytes accessed | tf_op | source)
XLA Modules:
  0.0 196.7 jit_solution(2243834859247009112)
XLA Ops:
  0.6 194.7 %qaoa.1 = (f32[8,1,128]{2,1,0:T(1,128)S(1)}, f32[8,2,2,64,128]{4,3,2,1,0:T(8,128)S(1)}, f32[8,2,2,64,128]{4,3,2,1,0:T(8,128)S(1)}) custom-call(f32[8,2,2,64,128]{4,3,2,1,0:T(8,128)} %bitcast.3, f32[8]{0:T(128)} %gammas_hbm.1, f32[8]{0:T(128)} %betas_hbm.1), custom_call_target="tpu_custom_call" | custom-call | tf_op jit(solution)/shard_map/qaoa/pallas_call | solution.py:403
  195.3 1.4 write_out.1

commit v20 on v17

--- a/solution.py
+++ b/solution.py
@@ -322,28 +322,49 @@
     cos_half, sin_half = half_angle(LAYERS - 1)
     energy_part[...] = jnp.zeros((8, LANES), jnp.float32)
 
+    def slot_gates(a, b, sub, i):
+        return rotate(*[[recv[0, a, b, sub, o, c, rows_of(i), :] for o in range(8)] for c in range(2)],
+                      cos_half, sin_half)
+
+    def early_half(a, carry):
+        def early_sub(sub, carry):
+            wait_all(recv, recv_sem, (0, a, 0, sub), 7)
+
+            def slots(i, carry):
+                for c, values in enumerate(slot_gates(a, 0, sub, i)):
+                    for o in range(8):
+                        recv[0, a, 0, sub, o, c, rows_of(i), :] = values[o]
+                return carry
+
+            lax.fori_loop(0, PER_SUB, slots, 0)
+            return carry
+
+        lax.fori_loop(0, SUB, early_sub, 0)
+        return carry
+
+    lax.fori_loop(0, 2, early_half, 0)
+
     def final_half(a, carry):
         def final_sub(sub, carry):
-            for b in range(2):
-                wait_all(recv, recv_sem, (0, a, b, sub), 7)
+            wait_all(recv, recv_sem, (0, a, 1, sub), 7)
 
             def slots(i, carry):
                 r = sub * PER_SUB + i
-                old = [[recv[0, a, b, sub, o, c, rows_of(i), :] for b in range(2) for o in range(8)]
-                       for c in range(2)]
-                re, im = rotate(*old, cos_half, sin_half)
+                re, im = slot_gates(a, 1, sub, i)
                 total = energy_part[...]
-                for b in range(2):
-                    for o in range(8):
+                for o in range(8):
+                    early = [recv[0, a, 0, sub, o, c, rows_of(i), :] for c in range(2)]
+                    pair_re, pair_im = rotate([early[0], re[o]], [early[1], im[o]], cos_half, sin_half)
+                    for b in range(2):
                         at = (block(o), a, b, rows_of(r))
-                        x, y = re[b * 8 + o], im[b * 8 + o]
+                        x, y = pair_re[b], pair_im[b]
                         out_re[at] = x
                         out_im[at] = y
                         total = total + cost[at] * (x * x + y * y)
                 energy_part[...] = total
                 return carry
 
-            lax.fori_loop(0, PER_SUB, slots, 0)
+            lax.fori_loop(0, PER_SUB, slots, 0, unroll=True)
             return carry
 
         lax.fori_loop(0, SUB, final_sub, 0)
@@ -361,14 +382,14 @@
                 for sub in range(SUB):
                     wait_all(send, send_sem, (par, a, b, sub), 7)
 
-    drain(1)
     for a in range(2):
         for sub in range(SUB):
             wait_bytes(cost.at[:, a, :, pl.ds(sub * 8 * PER_SUB, 8 * PER_SUB)], near_send.at[a, sub])
     wait_bytes(cost_swap.at[pl.ds(0, 6)], cost_send)
-    for offset in range(1, 8):
+    for offset in (7, 5, 6, 4, 3, 1, 2):
         remote(energy_row, energy_all.at[me], e_send.at[offset], e_recv.at[offset], offset)
     drain(0)
+    drain(1)
     for offset in range(1, 8):
         wait_bytes(energy_row, e_send.at[offset])
         wait_bytes(energy_row, e_recv.at[offset])

time: 197 us -> 197 us (level)
  no operation moved by 1% of the time
where the time goes in v20:
time: 197 us
  Pallas kernels  196 us (99%)
    pallas_call x1, Pallas kernels, device_body(): pl.pallas_call(kernel, out_shape=(pltpu.VMEM((8, 1, LANES), f32), pltpu.V...  195 us

profile of v20, /device:TPU:0, one launch (start us, length us, event | category | flops | bytes accessed | tf_op | source)
XLA Modules:
  0.0 196.6 jit_solution(13896733334700036712)
XLA Ops:
  0.6 194.6 %qaoa.1 = (f32[8,1,128]{2,1,0:T(1,128)S(1)}, f32[8,2,2,64,128]{4,3,2,1,0:T(8,128)S(1)}, f32[8,2,2,64,128]{4,3,2,1,0:T(8,128)S(1)}) custom-call(f32[8,2,2,64,128]{4,3,2,1,0:T(8,128)} %bitcast.3, f32[8]{0:T(128)} %gammas_hbm.1, f32[8]{0:T(128)} %betas_hbm.1), custom_call_target="tpu_custom_call" | custom-call | tf_op jit(solution)/shard_map/qaoa/pallas_call | solution.py:423
  195.2 1.4 write_out.1

commit v21 on v20

--- a/solution.py
+++ b/solution.py
@@ -351,7 +351,7 @@
             def slots(i, carry):
                 r = sub * PER_SUB + i
                 re, im = slot_gates(a, 1, sub, i)
-                total = energy_part[...]
+                terms = []
                 for o in range(8):
                     early = [recv[0, a, 0, sub, o, c, rows_of(i), :] for c in range(2)]
                     pair_re, pair_im = rotate([early[0], re[o]], [early[1], im[o]], cos_half, sin_half)
@@ -360,8 +360,10 @@
                         x, y = pair_re[b], pair_im[b]
                         out_re[at] = x
                         out_im[at] = y
-                        total = total + cost[at] * (x * x + y * y)
-                energy_part[...] = total
+                        terms.append(cost[at] * (x * x + y * y))
+                while len(terms) > 1:
+                    terms = [terms[k] + terms[k + 1] for k in range(0, len(terms), 2)]
+                energy_part[...] = energy_part[...] + terms[0]
                 return carry
 
             lax.fori_loop(0, PER_SUB, slots, 0, unroll=True)

time: 197 us -> 197 us (level)
  no operation moved by 1% of the time
where the time goes in v21:
time: 197 us
  Pallas kernels  196 us (99%)
    pallas_call x1, Pallas kernels, device_body(): pl.pallas_call(kernel, out_shape=(pltpu.VMEM((8, 1, LANES), f32), pltpu.V...  195 us

profile of v21, /device:TPU:0, one launch (start us, length us, event | category | flops | bytes accessed | tf_op | source)
XLA Modules:
  0.0 196.6 jit_solution(18154059883615842119)
XLA Ops:
  0.6 194.6 %qaoa.1 = (f32[8,1,128]{2,1,0:T(1,128)S(1)}, f32[8,2,2,64,128]{4,3,2,1,0:T(8,128)S(1)}, f32[8,2,2,64,128]{4,3,2,1,0:T(8,128)S(1)}) custom-call(f32[8,2,2,64,128]{4,3,2,1,0:T(8,128)} %bitcast.3, f32[8]{0:T(128)} %gammas_hbm.1, f32[8]{0:T(128)} %betas_hbm.1), custom_call_target="tpu_custom_call" | custom-call | tf_op jit(solution)/shard_map/qaoa/pallas_call | solution.py:425
  195.2 1.4 write_out.1

commit v22 on v20

--- a/solution.py
+++ b/solution.py
@@ -197,10 +197,13 @@
                 bit = NEAR[a]
                 part = cost_near.at[:, a, :, sub_rows(sub)]
                 wait_bytes(part, near_recv.at[a, sub])
-                for o in range(1, 8):
-                    if not o & bit:
-                        remote(cost_near.at[block(o), a, :, sub_rows(sub)],
-                               cost_swap.at[o | bit, a, :, sub_rows(sub)], cost_send, cost_recv, o)
+                @pl.when(sub % 2 == 1)
+                def _():
+                    rows = pl.ds(pl.multiple_of((sub - 1) * 8 * PER_SUB, 8), 16 * PER_SUB)
+                    for o in range(1, 8):
+                        if not o & bit:
+                            remote(cost_near.at[block(o), a, :, rows], cost_swap.at[o | bit, a, :, rows],
+                                   cost_send, cost_recv, o)
 
                 def slots(i, carry):
                     r = sub * PER_SUB + i

time: 197 us -> 197 us (level)
  no operation moved by 1% of the time
where the time goes in v22:
time: 197 us
  Pallas kernels  196 us (99%)
    pallas_call x1, Pallas kernels, device_body(): pl.pallas_call(kernel, out_shape=(pltpu.VMEM((8, 1, LANES), f32), pltpu.V...  195 us

profile of v22, /device:TPU:0, one launch (start us, length us, event | category | flops | bytes accessed | tf_op | source)
XLA Modules:
  0.0 196.6 jit_solution(10313095055763473792)
XLA Ops:
  0.6 194.6 %qaoa.1 = (f32[8,1,128]{2,1,0:T(1,128)S(1)}, f32[8,2,2,64,128]{4,3,2,1,0:T(8,128)S(1)}, f32[8,2,2,64,128]{4,3,2,1,0:T(8,128)S(1)}) custom-call(f32[8,2,2,64,128]{4,3,2,1,0:T(8,128)} %bitcast.3, f32[8]{0:T(128)} %gammas_hbm.1, f32[8]{0:T(128)} %betas_hbm.1), custom_call_target="tpu_custom_call" | custom-call | tf_op jit(solution)/shard_map/qaoa/pallas_call | solution.py:426
  195.2 1.4 write_out.1

commit v23 on v20

--- a/solution.py
+++ b/solution.py
@@ -387,12 +387,11 @@
             wait_bytes(cost.at[:, a, :, pl.ds(sub * 8 * PER_SUB, 8 * PER_SUB)], near_send.at[a, sub])
     wait_bytes(cost_swap.at[pl.ds(0, 6)], cost_send)
     for offset in (7, 5, 6, 4, 3, 1, 2):
-        remote(energy_row, energy_all.at[me], e_send.at[offset], e_recv.at[offset], offset)
+        remote(energy_row, energy_all.at[me], e_send, e_recv, offset)
     drain(0)
     drain(1)
-    for offset in range(1, 8):
-        wait_bytes(energy_row, e_send.at[offset])
-        wait_bytes(energy_row, e_recv.at[offset])
+    wait_bytes(energy_all.at[pl.ds(0, 7)], e_send)
+    wait_bytes(energy_all.at[pl.ds(0, 7)], e_recv)
 
 
 def write_out(energy_all, in_re, in_im, energy, out_re, out_im, value, sem):
@@ -436,7 +435,7 @@
                 pltpu.SMEM((LAYERS,), f32), pltpu.SMEM((LAYERS,), f32), dma((2,)), pltpu.SemaphoreType.REGULAR((2,)),
                 dma((SUB,)), dma((2, SUB)), dma((2, SUB)), dma, dma,
                 dma((2, 2, 2, SUB)), dma((2, 2, 2, SUB)),
-                dma((8,)), dma((8,)),
+                dma, dma,
             ],
             compiler_params=pltpu.CompilerParams(collective_id=0, has_side_effects=True),
             name='qaoa',

time: 197 us -> 197 us (level)
  no operation moved by 1% of the time
where the time goes in v23:
time: 197 us; the launch traced here: 196 us
  Pallas kernels  196 us (99%)
    pallas_call x1, Pallas kernels, device_body(): pl.pallas_call(kernel, out_shape=(pltpu.VMEM((8, 1, LANES), f32), pltpu.V...  194 us

profile of v23, /device:TPU:0, one launch (start us, length us, event | category | flops | bytes accessed | tf_op | source)
XLA Modules:
  0.0 196.5 jit_solution(17973116567536085116)
XLA Ops:
  0.6 194.5 %qaoa.1 = (f32[8,1,128]{2,1,0:T(1,128)S(1)}, f32[8,2,2,64,128]{4,3,2,1,0:T(8,128)S(1)}, f32[8,2,2,64,128]{4,3,2,1,0:T(8,128)S(1)}) custom-call(f32[8,2,2,64,128]{4,3,2,1,0:T(8,128)} %bitcast.3, f32[8]{0:T(128)} %gammas_hbm.1, f32[8]{0:T(128)} %betas_hbm.1), custom_call_target="tpu_custom_call" | custom-call | tf_op jit(solution)/shard_map/qaoa/pallas_call | solution.py:422
  195.1 1.4 write_out.1

commit v24 on v23

--- a/solution.py
+++ b/solution.py
@@ -165,7 +165,7 @@
             loads[sub].wait()
             for a in range(2):
                 remote(cost.at[:, a, :, sub_rows(sub)], cost_near.at[:, a, :, sub_rows(sub)],
-                       near_send.at[a, sub], near_recv.at[a, sub], NEAR[a])
+                       near_send, near_recv.at[a, sub], NEAR[a])
         signal_next(near_in.at[0])
         for load in angle_loads:
             load.wait()
@@ -382,9 +382,7 @@
                 for sub in range(SUB):
                     wait_all(send, send_sem, (par, a, b, sub), 7)
 
-    for a in range(2):
-        for sub in range(SUB):
-            wait_bytes(cost.at[:, a, :, pl.ds(sub * 8 * PER_SUB, 8 * PER_SUB)], near_send.at[a, sub])
+    wait_bytes(cost, near_send)
     wait_bytes(cost_swap.at[pl.ds(0, 6)], cost_send)
     for offset in (7, 5, 6, 4, 3, 1, 2):
         remote(energy_row, energy_all.at[me], e_send, e_recv, offset)
@@ -433,7 +431,7 @@
                 pltpu.VMEM((4 * LANES, 2 * LANES), f32), pltpu.VMEM((2 * LANES, 2 * LANES), f32),
                 pltpu.VMEM((8, LANES), f32), pltpu.VMEM((1, LANES), f32),
                 pltpu.SMEM((LAYERS,), f32), pltpu.SMEM((LAYERS,), f32), dma((2,)), pltpu.SemaphoreType.REGULAR((2,)),
-                dma((SUB,)), dma((2, SUB)), dma((2, SUB)), dma, dma,
+                dma((SUB,)), dma, dma((2, SUB)), dma, dma,
                 dma((2, 2, 2, SUB)), dma((2, 2, 2, SUB)),
                 dma, dma,
             ],

time: 197 us -> 196 us (level)
  no operation moved by 1% of the time
where the time goes in v24:
time: 196 us
  Pallas kernels  196 us (100%)
    pallas_call x1, Pallas kernels, device_body(): pl.pallas_call(kernel, out_shape=(pltpu.VMEM((8, 1, LANES), f32), pltpu.V...  194 us

profile of v24, /device:TPU:0, one launch (start us, length us, event | category | flops | bytes accessed | tf_op | source)
XLA Modules:
  0.0 196.4 jit_solution(7839760586140036718)
XLA Ops:
  0.6 194.4 %qaoa.1 = (f32[8,1,128]{2,1,0:T(1,128)S(1)}, f32[8,2,2,64,128]{4,3,2,1,0:T(8,128)S(1)}, f32[8,2,2,64,128]{4,3,2,1,0:T(8,128)S(1)}) custom-call(f32[8,2,2,64,128]{4,3,2,1,0:T(8,128)} %bitcast.3, f32[8]{0:T(128)} %gammas_hbm.1, f32[8]{0:T(128)} %betas_hbm.1), custom_call_target="tpu_custom_call" | custom-call | tf_op jit(solution)/shard_map/qaoa/pallas_call | solution.py:420
  195.0 1.4 write_out.1

commit v25 on v24

--- a/solution.py
+++ b/solution.py
@@ -383,11 +383,11 @@
                     wait_all(send, send_sem, (par, a, b, sub), 7)
 
     wait_bytes(cost, near_send)
-    wait_bytes(cost_swap.at[pl.ds(0, 6)], cost_send)
     for offset in (7, 5, 6, 4, 3, 1, 2):
         remote(energy_row, energy_all.at[me], e_send, e_recv, offset)
     drain(0)
     drain(1)
+    wait_bytes(cost_swap.at[pl.ds(0, 6)], cost_send)
     wait_bytes(energy_all.at[pl.ds(0, 7)], e_send)
     wait_bytes(energy_all.at[pl.ds(0, 7)], e_recv)
 

time: 196 us -> 196 us (level)
  no operation moved by 1% of the time
where the time goes in v25:
time: 196 us
  Pallas kernels  196 us (100%)
    pallas_call x1, Pallas kernels, device_body(): pl.pallas_call(kernel, out_shape=(pltpu.VMEM((8, 1, LANES), f32), pltpu.V...  194 us

profile of v25, /device:TPU:0, one launch (start us, length us, event | category | flops | bytes accessed | tf_op | source)
XLA Modules:
  0.0 196.4 jit_solution(414321171687725292)
XLA Ops:
  0.6 194.4 %qaoa.1 = (f32[8,1,128]{2,1,0:T(1,128)S(1)}, f32[8,2,2,64,128]{4,3,2,1,0:T(8,128)S(1)}, f32[8,2,2,64,128]{4,3,2,1,0:T(8,128)S(1)}) custom-call(f32[8,2,2,64,128]{4,3,2,1,0:T(8,128)} %bitcast.3, f32[8]{0:T(128)} %gammas_hbm.1, f32[8]{0:T(128)} %betas_hbm.1), custom_call_target="tpu_custom_call" | custom-call | tf_op jit(solution)/shard_map/qaoa/pallas_call | solution.py:420
  195.0 1.4 write_out.1
